TPU v7x, 256 devices: a whole 4x4x8 slice. The times are simulated.
256 devices in a mesh: row: 8 (over z_lo, x), col: 32 (over z_hi, y, core).
Axes of the slice: x: 4, y: 4, z: 8 (z_hi: 4, z_lo: 2; z = z_hi * 2 + z_lo), core: 2. Of those that a mesh axis runs over, the one named last changes fastest.
Arguments:
- upper_a: float32 [4, 8, 256, 32, 256], P(None, 'row', None, 'col'), may hold values from -0.375 to 0.375
- upper_b: float32 [4, 8, 256, 32, 256], P(None, 'row', None, 'col'), may hold values from -0.375 to 0.375
- right_side: float32 [4, 8, 256, 32, 256], P(None, 'row', None, 'col'), may hold values from -6 to 6
- vectors_a: float32 [4, 8, 256, 256], P(None, 'row'), may hold values from -0.375 to 0.375
- inverse_a: float32 [4, 8, 256, 256], P(None, 'row'), may hold values from -0.375 to 0.375
- values_a: float32 [4, 8, 256], P(None, 'row'), may hold values from 0.5 to 2
- vectors_b: float32 [32, 256, 256], P('col'), may hold values from -0.375 to 0.375
- inverse_b: float32 [32, 256, 256], P('col'), may hold values from -0.375 to 0.375
- values_b: float32 [32, 256], P('col'), may hold values from 0.5 to 2
Outputs:
- solved: float32 [4, 8, 256, 32, 256], P(None, 'row', None, 'col')
All inputs are finite; a program needn't handle non-finite values.
Results may differ from a plain program's by a relative error of at most 0.0001.
Values sent between devices are 32-bit elements; how exact they have to be, the bound alone decides.
A program may use at most 64 MiB of HBM per device.

v0:
```python
import jax
import jax.numpy as jnp
from jax import lax
from jax.sharding import Mesh
from jax.sharding import PartitionSpec as P

FRONTS = 4
COL = ("col_0", "col_1", "col_2")


EXACT = lax.Precision.HIGHEST


def passed_along(value, axis, by):
    length = lax.axis_size(axis)
    pairs = [(i, i + by) for i in range(length) if 0 <= i + by < length]
    return lax.ppermute(value, axis, pairs)


def shifted(value, axis, steps):
    count = lax.axis_size(axis)
    pairs = [(source, (source + steps) % count) for source in range(count)]
    return lax.ppermute(value, axis, pairs)


def broadcast(value, axis, root):
    return lax.dynamic_index_in_dim(lax.all_gather(value, axis), root, 0, keepdims=False)


def rows_for(lines, length):
    spare = -len(lines) % length
    return jnp.pad(lines, [(0, spare)] + [(0, 0)] * (lines.ndim - 1))


def sent_to_all(value, axis):
    length = lax.axis_size(axis)
    return lax.all_to_all(
        jnp.broadcast_to(value[None], (length, *value.shape)), axis, 0, 0, tiled=True
    )


def in_order(blocks, dim):
    shape = list(blocks.shape[1:])
    shape[dim] *= blocks.shape[0]
    return jnp.moveaxis(blocks, 0, dim).reshape(shape)


def gather_axes(value, axes, dim):
    far, near = axes
    blocks = sent_to_all(sent_to_all(value, far), near)
    return in_order(blocks.swapaxes(0, 1).reshape(-1, *value.shape), dim)


def split_up(value, dim, length):
    shape = value.shape
    blocks = value.reshape(*shape[:dim], length, shape[dim] // length, *shape[dim + 1 :])
    return jnp.moveaxis(blocks, dim, 0)


def sum_at_owner(value, axis, dim):
    length = lax.axis_size(axis)
    blocks = lax.all_to_all(split_up(value, dim, length), axis, 0, 0, tiled=True)
    return jnp.sum(blocks, axis=0)


def sum_in_two_steps(value, axes, dim):
    far, near = axes
    blocks = split_up(value, dim, lax.axis_size(far))
    nearer = sum_at_owner(blocks, near, dim + 1)
    arrived = lax.all_to_all(nearer, far, split_axis=0, concat_axis=0, tiled=True)
    return arrived.sum(axis=0)


def nested_sum(value, axes):
    lines = value.reshape(-1, value.shape[-1])
    padded = rows_for(lines, lax.axis_size(axes[0]) * lax.axis_size(axes[1]))
    whole = gather_axes(sum_in_two_steps(padded, axes, 0), axes, 0)
    return lax.slice_in_dim(whole, 0, len(lines)).reshape(value.shape)


def matmul(former, latter):
    return jnp.dot(former, latter, precision=EXACT, preferred_element_type=jnp.float32)


def diagonal_solve(residual, vectors_a, inverse_a, values_a, vectors_b, inverse_b, values_b):
    rotated = matmul(matmul(inverse_a, residual), vectors_b)
    scaled = rotated / (values_a[:, None] + values_b[None, :])
    return matmul(matmul(vectors_a, scaled), inverse_b)


def body(
    upper_a, upper_b, right_side, vectors_a, inverse_a, values_a, vectors_b, inverse_b, values_b
):
    row_count = lax.axis_size("row")
    col_count = lax.axis_size(COL)
    row_pos = lax.axis_index("row")
    col_pos = lax.axis_index(COL)
    local_blocks = right_side.shape[0]
    block_size = right_side.shape[2]
    square = (local_blocks, block_size, block_size)
    panel_a = upper_a.reshape(square)
    panel_b = upper_b.reshape(square)
    work = right_side.reshape(square)
    left_vectors = vectors_a.reshape(square)
    left_inverse = inverse_a.reshape(square)
    left_values = values_a.reshape(local_blocks, block_size)
    right_vectors = vectors_b.reshape(block_size, block_size)
    right_inverse = inverse_b.reshape(block_size, block_size)
    right_values = values_b.reshape(block_size)
    block_ids = jnp.arange(local_blocks, dtype=jnp.int32)
    global_rows = block_ids * row_count + row_pos
    offsets = list(range(-1, FRONTS - 1))
    moved_upper = {}
    for offset in offsets:
        if offset == 0:
            moved_upper[offset] = panel_a
        else:
            moved_upper[offset] = passed_along(panel_a, COL, offset)
    zero_block = jnp.zeros((1, block_size, block_size), jnp.float32)
    moved_lower = {}
    for offset in offsets:
        if offset % row_count == 0:
            arrived = panel_b
        else:
            arrived = shifted(panel_b, "row", -offset)
        block_carry = jnp.floor_divide(row_pos + offset, row_count)
        padded = jnp.concatenate([zero_block, arrived, zero_block], axis=0)
        moved_lower[offset] = lax.dynamic_slice_in_dim(padded, 1 + block_carry, local_blocks, 0)
    for offset in offsets:
        target = col_pos - offset
        slot_index = jnp.floor_divide(target - row_pos, row_count)
        present = (
            (jnp.remainder(target - row_pos, row_count) == 0) & (target >= 0) & (target < col_count)
        )
        picked = jnp.clip(slot_index, 0, local_blocks - 1)
        residual = lax.dynamic_index_in_dim(work, picked, 0, keepdims=False)
        solved = diagonal_solve(
            residual,
            lax.dynamic_index_in_dim(left_vectors, picked, 0, keepdims=False),
            lax.dynamic_index_in_dim(left_inverse, picked, 0, keepdims=False),
            lax.dynamic_index_in_dim(left_values, picked, 0, keepdims=False),
            right_vectors,
            right_inverse,
            right_values,
        )
        on_front = (block_ids == slot_index) & present
        work = jnp.where(on_front[:, None, None], solved[None], work)
        column_block = broadcast(solved, "row", jnp.remainder(target, row_count))
        upper_term = jnp.einsum("qab,bc->qac", moved_upper[offset], column_block, precision=EXACT)
        slot_blocks = jnp.where(on_front[:, None, None], solved[None], jnp.zeros_like(work))
        row_solved = nested_sum(slot_blocks, (("col_0", "col_1"), "col_2"))
        lower_term = jnp.einsum("qab,qbc->qac", row_solved, moved_lower[offset], precision=EXACT)
        pending = col_pos - global_rows > offset
        work = jnp.where(pending[:, None, None], work - (upper_term + lower_term), work)
    return work.reshape(right_side.shape)


def solution(mesh):
    finer = Mesh(
        mesh.devices.reshape(mesh.shape["row"], 4, 4, 2), ("row", "col_0", "col_1", "col_2")
    )
    placed = (
        P(None, "row", None, COL, None),
        P(None, "row", None, COL, None),
        P(None, "row", None, COL, None),
        P(None, "row", None, None),
        P(None, "row", None, None),
        P(None, "row", None),
        P(COL, None, None),
        P(COL, None, None),
        P(COL, None),
    )
    return jax.shard_map(
        body,
        mesh=finer,
        in_specs=placed,
        out_specs=P(None, "row", None, COL, None),
        check_vma=False,
    )
```

profile of v0, /device:TPU:192, one launch (start us, length us, event | category | flops | bytes accessed | tf_op | source)
XLA Modules:
  0.0 436.9 jit_solution(6439170604961360345)
XLA Ops:
  14.3 4.6 %all_to_all.80 = f32[2,16,32,256]{3,2,1,0:T(8,128)S(1)} all-to-all(f32[2,16,32,256]{3,2,1,0:T(8,128)S(1)} %copy.72), channel_id=1, replica_groups=mesh['row'=8,'col_0'=4,'col_1'=4,'col_2'=2] {'col_2'}, dimensions={0} | all-to-all | bytes 2097152 | tf_op jit(solution)/shard_map/all_to_all | solution.py:62
  19.8 9.0 %all-to-all-start.1 = ((f32[16,32,256]{2,1,0:T(8,128)}), f32[16,32,256]{2,1,0:T(8,128)S(1)}, u32[]{:S(2)}, u32[]{:S(2)}) async-start(f32[16,32,256]{2,1,0:T(8,128)} %reduce_sum.72), calls=%async_computation.1 | async-start | bytes 1048576 | tf_op jit(solution)/shard_map/all_to_all | solution.py:70
  31.7 19.2 %all-to-all-done.1 = f32[16,32,256]{2,1,0:T(8,128)S(1)} async-done(((f32[16,32,256]{2,1,0:T(8,128)}), f32[16,32,256]{2,1,0:T(8,128)S(1)}, u32[]{:S(2)}, u32[]{:S(2)}) %all-to-all-start.1) | async-done | bytes 524320 | tf_op jit(solution)/shard_map/all_to_all | solution.py:70
  51.7 5.6 %all-to-all-start.2 = ((f32[16,32,256]{2,1,0:T(8,128)}), f32[16,32,256]{2,1,0:T(8,128)S(1)}, u32[]{:S(2)}, u32[]{:S(2)}) async-start(f32[16,32,256]{2,1,0:T(8,128)} %broadcast_in_dim.222), calls=%async_computation.2 | async-start | bytes 1048576 | tf_op jit(solution)/shard_map/all_to_all | solution.py:37
  68.3 9.0 %all-to-all-done.2 = f32[16,32,256]{2,1,0:T(8,128)S(1)} async-done(((f32[16,32,256]{2,1,0:T(8,128)}), f32[16,32,256]{2,1,0:T(8,128)S(1)}, u32[]{:S(2)}, u32[]{:S(2)}) %all-to-all-start.2) | async-done | bytes 524320 | tf_op jit(solution)/shard_map/all_to_all | solution.py:37
  77.4 4.6 %all_to_all.81 = f32[2,16,32,256]{3,2,1,0:T(8,128)S(1)} all-to-all(f32[2,16,32,256]{3,2,1,0:T(8,128)S(1)} %broadcast_in_dim.223), channel_id=1, replica_groups=mesh['row'=8,'col_0'=4,'col_1'=4,'col_2'=2] {'col_2'}, dimensions={0} | all-to-all | bytes 2097152 | tf_op jit(solution)/shard_map/all_to_all | solution.py:37
  101.3 5.4 %all_to_all.82 = f32[2,16,32,256]{3,2,1,0:T(8,128)} all-to-all(f32[2,16,32,256]{3,2,1,0:T(8,128)S(1)} %copy.78), channel_id=1, replica_groups=mesh['row'=8,'col_0'=4,'col_1'=4,'col_2'=2] {'col_2'}, dimensions={0} | all-to-all | bytes 2097152 | tf_op jit(solution)/shard_map/all_to_all | solution.py:62
  108.9 34.0 %all_to_all.83 = f32[16,32,256]{2,1,0:T(8,128)S(1)} all-to-all(f32[16,32,256]{2,1,0:T(8,128)} %reduce_sum.74), channel_id=1, replica_groups=mesh['row'=8,'col_0'=4,'col_1'=4,'col_2'=2] {'col_0','col_1'}, dimensions={0} | all-to-all | bytes 1048576 | tf_op jit(solution)/shard_map/all_to_all | solution.py:70
  143.7 5.8 %all-to-all-start.6 = ((f32[16,32,256]{2,1,0:T(8,128)}), f32[16,32,256]{2,1,0:T(8,128)S(1)}, u32[]{:S(2)}, u32[]{:S(2)}) async-start(f32[16,32,256]{2,1,0:T(8,128)} %broadcast_in_dim.231), calls=%async_computation.6 | async-start | bytes 1048576 | tf_op jit(solution)/shard_map/all_to_all | solution.py:37
  150.4 14.4 %all-to-all-done.6 = f32[16,32,256]{2,1,0:T(8,128)S(1)} async-done(((f32[16,32,256]{2,1,0:T(8,128)}), f32[16,32,256]{2,1,0:T(8,128)S(1)}, u32[]{:S(2)}, u32[]{:S(2)}) %all-to-all-start.6) | async-done | bytes 524320 | tf_op jit(solution)/shard_map/all_to_all | solution.py:37
  165.0 4.7 %all_to_all.84 = f32[2,16,32,256]{3,2,1,0:T(8,128)S(1)} all-to-all(f32[2,16,32,256]{3,2,1,0:T(8,128)S(1)} %broadcast_in_dim.232), channel_id=1, replica_groups=mesh['row'=8,'col_0'=4,'col_1'=4,'col_2'=2] {'col_2'}, dimensions={0} | all-to-all | bytes 2097152 | tf_op jit(solution)/shard_map/all_to_all | solution.py:37
  184.2 5.5 %all_to_all.85 = f32[2,16,32,256]{3,2,1,0:T(8,128)} all-to-all(f32[2,16,32,256]{3,2,1,0:T(8,128)S(1)} %copy.84), channel_id=1, replica_groups=mesh['row'=8,'col_0'=4,'col_1'=4,'col_2'=2] {'col_2'}, dimensions={0} | all-to-all | bytes 2097152 | tf_op jit(solution)/shard_map/all_to_all | solution.py:62
  191.9 8.9 %all-to-all-start.9 = ((f32[16,32,256]{2,1,0:T(8,128)}), f32[16,32,256]{2,1,0:T(8,128)}, u32[]{:S(2)}, u32[]{:S(2)}) async-start(f32[16,32,256]{2,1,0:T(8,128)} %reduce_sum.76), calls=%async_computation.9 | async-start | bytes 1048576 | tf_op jit(solution)/shard_map/all_to_all | solution.py:70
  200.8 14.0 %collective-permute-start.3 = (f32[4,256,256]{2,1,0:T(8,128)S(1)}, f32[4,256,256]{2,1,0:T(8,128)}, u32[]{:S(2)}, u32[]{:S(2)}) collective-permute-start(f32[4,256,256]{2,1,0:T(8,128)S(1)} %bitcast.159), channel_id=1, source_target_pairs={{0,224},{32,0},{64,32},{96,64},{128,96},{160,128},{192,160},{224,1... | collective-permute-start | bytes 3145736 | tf_op jit(solution)/shard_map/ppermute | solution.py:23
  214.8 6.8 %all-to-all-done.9 = f32[16,32,256]{2,1,0:T(8,128)} async-done(((f32[16,32,256]{2,1,0:T(8,128)}), f32[16,32,256]{2,1,0:T(8,128)}, u32[]{:S(2)}, u32[]{:S(2)}) %all-to-all-start.9) | async-done | bytes 524320 | tf_op jit(solution)/shard_map/all_to_all | solution.py:70
  223.5 5.9 %all-to-all-start.10 = ((f32[16,32,256]{2,1,0:T(8,128)}), f32[16,32,256]{2,1,0:T(8,128)}, u32[]{:S(2)}, u32[]{:S(2)}) async-start(f32[16,32,256]{2,1,0:T(8,128)} %broadcast_in_dim.239), calls=%async_computation.10 | async-start | bytes 1048576 | tf_op jit(solution)/shard_map/all_to_all | solution.py:37
  233.2 47.6 %all-to-all-done.10 = f32[16,32,256]{2,1,0:T(8,128)} async-done(((f32[16,32,256]{2,1,0:T(8,128)}), f32[16,32,256]{2,1,0:T(8,128)}, u32[]{:S(2)}, u32[]{:S(2)}) %all-to-all-start.10) | async-done | bytes 524320 | tf_op jit(solution)/shard_map/all_to_all | solution.py:37
  282.1 4.6 %all_to_all.86 = f32[2,16,32,256]{3,2,1,0:T(8,128)S(1)} all-to-all(f32[2,16,32,256]{3,2,1,0:T(8,128)S(1)} %broadcast_in_dim.240), channel_id=1, replica_groups=mesh['row'=8,'col_0'=4,'col_1'=4,'col_2'=2] {'col_2'}, dimensions={0} | all-to-all | bytes 2097152 | tf_op jit(solution)/shard_map/all_to_all | solution.py:37
  301.5 5.5 %all_to_all.87 = f32[2,16,32,256]{3,2,1,0:T(8,128)} all-to-all(f32[2,16,32,256]{3,2,1,0:T(8,128)S(1)} %copy.90), channel_id=1, replica_groups=mesh['row'=8,'col_0'=4,'col_1'=4,'col_2'=2] {'col_2'}, dimensions={0} | all-to-all | bytes 2097152 | tf_op jit(solution)/shard_map/all_to_all | solution.py:62
  309.2 5.5 %all-to-all-start.13 = ((f32[16,32,256]{2,1,0:T(8,128)}), f32[16,32,256]{2,1,0:T(8,128)}, u32[]{:S(2)}, u32[]{:S(2)}) async-start(f32[16,32,256]{2,1,0:T(8,128)} %reduce_sum.78), calls=%async_computation.13 | async-start | bytes 1048576 | tf_op jit(solution)/shard_map/all_to_all | solution.py:70
  314.8 20.1 %all-to-all-done.13 = f32[16,32,256]{2,1,0:T(8,128)} async-done(((f32[16,32,256]{2,1,0:T(8,128)}), f32[16,32,256]{2,1,0:T(8,128)}, u32[]{:S(2)}, u32[]{:S(2)}) %all-to-all-start.13) | async-done | bytes 524320 | tf_op jit(solution)/shard_map/all_to_all | solution.py:70
  336.8 6.3 %all-to-all-start.14 = ((f32[16,32,256]{2,1,0:T(8,128)}), f32[16,32,256]{2,1,0:T(8,128)}, u32[]{:S(2)}, u32[]{:S(2)}) async-start(f32[16,32,256]{2,1,0:T(8,128)} %broadcast_in_dim.247), calls=%async_computation.14 | async-start | bytes 1048576 | tf_op jit(solution)/shard_map/all_to_all | solution.py:37
  348.3 51.2 %all-to-all-done.14 = f32[16,32,256]{2,1,0:T(8,128)} async-done(((f32[16,32,256]{2,1,0:T(8,128)}), f32[16,32,256]{2,1,0:T(8,128)}, u32[]{:S(2)}, u32[]{:S(2)}) %all-to-all-start.14) | async-done | bytes 524320 | tf_op jit(solution)/shard_map/all_to_all | solution.py:37
  408.4 14.0 %collective-permute-done.4 = f32[4,256,256]{2,1,0:T(8,128)} collective-permute-done((f32[4,256,256]{2,1,0:T(8,128)}, f32[4,256,256]{2,1,0:T(8,128)}, u32[]{:S(2)}, u32[]{:S(2)}) %collective-permute-start.4) | collective-permute-done | bytes 1048608 | tf_op jit(solution)/shard_map/ppermute | solution.py:17
  (138 shorter events, 110.9 us)
Async XLA Ops:
  6.5 86.0 %all-gather.9.cloned.1.call-start = ((), (), s32[]{:S(2)}) async-start(), calls=%async_computation.16 | async-start | bytes 2359296 | tf_op jit(solution)/shard_map/all_gather | solution.py:27
  19.8 31.1 %all-to-all-start.1 = ((f32[16,32,256]{2,1,0:T(8,128)}), f32[16,32,256]{2,1,0:T(8,128)S(1)}, u32[]{:S(2)}, u32[]{:S(2)}) async-start(f32[16,32,256]{2,1,0:T(8,128)} %reduce_sum.72), calls=%async_computation.1 | async-start | bytes 1048576 | tf_op jit(solution)/shard_map/all_to_all | solution.py:70
  30.1 29.6 %copy-start.4 = (f32[4,1,256,1,256]{4,2,3,1,0:T(8,128)}, f32[4,1,256,1,256]{4,2,3,1,0:T(8,128)S(1)}, u32[]{:S(2)}) copy-start(f32[4,1,256,1,256]{4,2,3,1,0:T(8,128)S(1)} %copy.112) | copy-start | bytes 3145732
  30.1 33.7 %copy-start.8 = (f32[256,256]{1,0:T(8,128)S(1)}, f32[256,256]{1,0:T(8,128)}, u32[]{:S(2)}) copy-start(f32[256,256]{1,0:T(8,128)} %fusion.40) | copy-start | bytes 786436
  30.1 54.5 %collective-permute-start.1 = (f32[4,256,256]{2,1,0:T(8,128)S(1)}, f32[4,256,256]{2,1,0:T(8,128)}, u32[]{:S(2)}, u32[]{:S(2)}) collective-permute-start(f32[4,256,256]{2,1,0:T(8,128)S(1)} %bitcast.157), channel_id=1, source_target_pairs={{0,32},{32,64},{64,96},{96,128},{128,160},{160,192},{192,224},{224... | collective-permute-start | bytes 3145736 | tf_op jit(solution)/shard_map/ppermute | solution.py:23
  51.7 25.6 %all-to-all-start.2 = ((f32[16,32,256]{2,1,0:T(8,128)}), f32[16,32,256]{2,1,0:T(8,128)S(1)}, u32[]{:S(2)}, u32[]{:S(2)}) async-start(f32[16,32,256]{2,1,0:T(8,128)} %broadcast_in_dim.222), calls=%async_computation.2 | async-start | bytes 1048576 | tf_op jit(solution)/shard_map/all_to_all | solution.py:37
  57.4 115.8 %all-gather.11.cloned.1.call-start = ((), (), s32[]{:S(2)}) async-start(), calls=%async_computation.17 | async-start | bytes 2359296 | tf_op jit(solution)/shard_map/all_gather | solution.py:27
  59.7 32.8 %collective-permute-start = (f32[4,256,256]{2,1,0:T(8,128)}, f32[4,256,256]{2,1,0:T(8,128)}, u32[]{:S(2)}, u32[]{:S(2)}) collective-permute-start(f32[4,256,256]{2,1,0:T(8,128)} %bitcast.156), channel_id=1, source_target_pairs={{1,0},{2,1},{3,2},{4,3},{5,4},{6,5},{7,6},{8,7},{9,8},{10,9},{11,1... | collective-permute-start | bytes 3145736 | tf_op jit(solution)/shard_map/ppermute | solution.py:17
  84.6 7.9 %copy-start.11 = (f32[256,256]{0,1:T(8,128)S(1)}, f32[256,256]{0,1:T(8,128)}, u32[]{:S(2)}) copy-start(f32[256,256]{0,1:T(8,128)} %copy.68) | copy-start | bytes 786436
  106.7 42.9 %copy-start.9 = (f32[256,256]{1,0:T(8,128)S(1)}, f32[256,256]{1,0:T(8,128)}, u32[]{:S(2)}) copy-start(f32[256,256]{1,0:T(8,128)} %fusion.38) | copy-start | bytes 786436
  143.7 21.1 %all-to-all-start.6 = ((f32[16,32,256]{2,1,0:T(8,128)}), f32[16,32,256]{2,1,0:T(8,128)S(1)}, u32[]{:S(2)}, u32[]{:S(2)}) async-start(f32[16,32,256]{2,1,0:T(8,128)} %broadcast_in_dim.231), calls=%async_computation.6 | async-start | bytes 1048576 | tf_op jit(solution)/shard_map/all_to_all | solution.py:37
  149.5 143.6 %all-gather.13.cloned.1.call-start = ((), (), s32[]{:S(2)}) async-start(), calls=%async_computation.18 | async-start | bytes 2359296 | tf_op jit(solution)/shard_map/all_gather | solution.py:27
  165.0 8.1 %copy-start.10 = (f32[4,1,256,1,256]{4,3,2,1,0:T(1,128)S(1)}, f32[4,1,256,1,256]{4,3,2,1,0:T(1,128)}, u32[]{:S(2)}) copy-start(f32[4,1,256,1,256]{4,3,2,1,0:T(1,128)} %param.9) | copy-start | bytes 3145732
  184.2 16.6 %copy-start.5 = (f32[4,1,256,1,256]{4,2,3,1,0:T(8,128)S(1)}, f32[4,1,256,1,256]{4,2,3,1,0:T(8,128)}, u32[]{:S(2)}) copy-start(f32[4,1,256,1,256]{4,2,3,1,0:T(8,128)} %copy-done.4) | copy-start | bytes 3145732
  191.9 29.7 %all-to-all-start.9 = ((f32[16,32,256]{2,1,0:T(8,128)}), f32[16,32,256]{2,1,0:T(8,128)}, u32[]{:S(2)}, u32[]{:S(2)}) async-start(f32[16,32,256]{2,1,0:T(8,128)} %reduce_sum.76), calls=%async_computation.9 | async-start | bytes 1048576 | tf_op jit(solution)/shard_map/all_to_all | solution.py:70
  200.8 85.9 %collective-permute-start.3 = (f32[4,256,256]{2,1,0:T(8,128)S(1)}, f32[4,256,256]{2,1,0:T(8,128)}, u32[]{:S(2)}, u32[]{:S(2)}) collective-permute-start(f32[4,256,256]{2,1,0:T(8,128)S(1)} %bitcast.159), channel_id=1, source_target_pairs={{0,224},{32,0},{64,32},{96,64},{128,96},{160,128},{192,160},{224,1... | collective-permute-start | bytes 3145736 | tf_op jit(solution)/shard_map/ppermute | solution.py:23
  223.5 57.4 %all-to-all-start.10 = ((f32[16,32,256]{2,1,0:T(8,128)}), f32[16,32,256]{2,1,0:T(8,128)}, u32[]{:S(2)}, u32[]{:S(2)}) async-start(f32[16,32,256]{2,1,0:T(8,128)} %broadcast_in_dim.239), calls=%async_computation.10 | async-start | bytes 1048576 | tf_op jit(solution)/shard_map/all_to_all | solution.py:37
  229.5 192.9 %all-gather.15.cloned.1.call-start = ((), (), s32[]{:S(2)}) async-start(), calls=%async_computation.19 | async-start | bytes 2359296 | tf_op jit(solution)/shard_map/all_gather | solution.py:27
  229.5 63.6 %collective-permute-start.2 = (f32[4,256,256]{2,1,0:T(8,128)}, f32[4,256,256]{2,1,0:T(8,128)}, u32[]{:S(2)}, u32[]{:S(2)}) collective-permute-start(f32[4,256,256]{2,1,0:T(8,128)} %bitcast.156), channel_id=1, source_target_pairs={{0,1},{1,2},{2,3},{3,4},{4,5},{5,6},{6,7},{7,8},{8,9},{9,10},{10,1... | collective-permute-start | bytes 3145736 | tf_op jit(solution)/shard_map/ppermute | solution.py:17
  301.5 13.2 %copy-start.6 = (f32[4,1,256,1,256]{4,2,3,1,0:T(8,128)S(1)}, f32[4,1,256,1,256]{4,2,3,1,0:T(8,128)}, u32[]{:S(2)}) copy-start(f32[4,1,256,1,256]{4,2,3,1,0:T(8,128)} %copy-done.4) | copy-start | bytes 3145732
  309.2 25.7 %all-to-all-start.13 = ((f32[16,32,256]{2,1,0:T(8,128)}), f32[16,32,256]{2,1,0:T(8,128)}, u32[]{:S(2)}, u32[]{:S(2)}) async-start(f32[16,32,256]{2,1,0:T(8,128)} %reduce_sum.78), calls=%async_computation.13 | async-start | bytes 1048576 | tf_op jit(solution)/shard_map/all_to_all | solution.py:70
  314.7 90.5 %collective-permute-start.5 = (f32[4,256,256]{2,1,0:T(8,128)S(1)}, f32[4,256,256]{2,1,0:T(8,128)}, u32[]{:S(2)}, u32[]{:S(2)}) collective-permute-start(f32[4,256,256]{2,1,0:T(8,128)S(1)} %bitcast.160), channel_id=1, source_target_pairs={{0,192},{32,224},{64,0},{96,32},{128,64},{160,96},{192,128},{224,1... | collective-permute-start | bytes 3145736 | tf_op jit(solution)/shard_map/ppermute | solution.py:23
  336.8 62.6 %all-to-all-start.14 = ((f32[16,32,256]{2,1,0:T(8,128)}), f32[16,32,256]{2,1,0:T(8,128)}, u32[]{:S(2)}, u32[]{:S(2)}) async-start(f32[16,32,256]{2,1,0:T(8,128)} %broadcast_in_dim.247), calls=%async_computation.14 | async-start | bytes 1048576 | tf_op jit(solution)/shard_map/all_to_all | solution.py:37
  343.1 79.3 %collective-permute-start.4 = (f32[4,256,256]{2,1,0:T(8,128)}, f32[4,256,256]{2,1,0:T(8,128)}, u32[]{:S(2)}, u32[]{:S(2)}) collective-permute-start(f32[4,256,256]{2,1,0:T(8,128)} %bitcast.156), channel_id=1, source_target_pairs={{0,2},{1,3},{2,4},{3,5},{4,6},{5,7},{6,8},{7,9},{8,10},{9,11},{10,... | collective-permute-start | bytes 3145736 | tf_op jit(solution)/shard_map/ppermute | solution.py:17
  (10 other events, 33.3 us)
Sparse Core Ops, SparseCore 0:
  12.9 60.8 all-gather.8
  99.9 73.1 all-gather.10
  182.9 72.1 all-gather.12
  300.2 53.6 all-gather.14
where the time goes:
time: 439 us; the launch traced here: 437 us
  waiting for transfers between devices  193 us (44%)
  blocking collectives  73.4 us (17%)
  starting transfers between devices  72.2 us (16%)
  matrix products  43.4 us (10%)
  local copies, waits for them, and re-layouts  30.6 us (7%)
  between operations  13.9 us (3%)
  other arithmetic  10.2 us (2%)
    all_to_all x4, waiting for transfers between devices, sent_to_all(): lax.all_to_all(jnp.broadcast_to(value[None], (length, *value.shape)), axi...  122 us
    all_to_all x3, waiting for transfers between devices, sum_in_two_steps(): lax.all_to_all(nearer, far, split_axis=0, concat_axis=0, tiled=True)  46 us
    all_to_all x1, blocking collectives, sum_in_two_steps(): lax.all_to_all(nearer, far, split_axis=0, concat_axis=0, tiled=True)  34 us
    all_to_all x4, starting transfers between devices, sent_to_all(): lax.all_to_all(jnp.broadcast_to(value[None], (length, *value.shape)), axi...  23.6 us
    all_to_all x3, starting transfers between devices, sum_in_two_steps(): lax.all_to_all(nearer, far, split_axis=0, concat_axis=0, tiled=True)  23.4 us
    all_to_all x4, blocking collectives, sum_at_owner(): lax.all_to_all(split_up(value, dim, length), axis, 0, 0, tiled=True)  21 us
    ppermute x3, waiting for transfers between devices, passed_along(): return lax.ppermute(value, axis, pairs)  20 us
    all_to_all x4, blocking collectives, sent_to_all(): lax.all_to_all(jnp.broadcast_to(value[None], (length, *value.shape)), axi...  18.4 us
  transfers between devices with their start and end apart: 17, of which 12 were waited for; matrix products, arithmetic and copies ran while one was open for 11% of the time, Pallas kernels for 0%

commit v1 on v0

v1 whole, which is shorter than its diff:
```python
import functools

import jax
import jax.numpy as jnp
from jax import lax
from jax.experimental import pallas as pl
from jax.experimental.pallas import tpu as pltpu
from jax.sharding import Mesh
from jax.sharding import PartitionSpec as P

FRONTS = 4
N_SLOT = 4
BLOCK = 256
HALF = 128
N_COL = 32
MESH = pl.DeviceIdType.MESH
ROW = ("zl", "x")
COL = ("zh", "y", "k")


def parts(value):
    high = value.astype(jnp.bfloat16)
    low = (value - high.astype(jnp.float32)).astype(jnp.bfloat16)
    return high, low


def matmul(former, latter):
    former_high, former_low = parts(former)
    latter_high, latter_low = parts(latter)
    left = jnp.concatenate([former_high, former_low, former_high], axis=1)
    right = jnp.concatenate([latter_high, latter_high, latter_low], axis=0)
    return jnp.dot(left, right, preferred_element_type=jnp.float32)


def kernel(
    a_hbm, b_hbm, w_hbm, va_hbm, ia_hbm, la_ref, vb_hbm, ib_hbm, lb_ref, out_hbm,
    a_all, b_all, work, x_col, x_row, va, ia, vb, ib, denominator,
    a_send, a_recv, b_send, b_recv, row_send, row_far, row_recv, col_send, col_recv, local, out_sem,
):
    zl, x = lax.axis_index("zl"), lax.axis_index("x")
    zh, y, k = lax.axis_index("zh"), lax.axis_index("y"), lax.axis_index("k")
    r = zl * 4 + x
    c = zh * 8 + y * 2 + k
    rem, div = lax.rem, lax.div

    def place(zl=zl, x=x, zh=zh, y=y, k=k):
        return {"zl": zl, "x": x, "zh": zh, "y": y, "k": k}

    def at_column(j):
        return place(zh=div(j, 8), y=div(rem(j, 8), 2), k=rem(j, 2))

    def at_row(i):
        return place(zl=div(i, 4), x=rem(i, 4))

    def remote(src, dst, send_sem, recv_sem, where):
        return pltpu.make_async_remote_copy(
            src_ref=src, dst_ref=dst, send_sem=send_sem, recv_sem=recv_sem,
            device_id=where, device_id_type=MESH,
        )

    own_front = rem(c - r + 33, 8)
    own_slot = div(c - r - own_front + 1 + 64, 8) - 8
    owner = (own_front < FRONTS) & (own_slot >= 0) & (own_slot < N_SLOT)
    slot = jnp.clip(own_slot, 0, N_SLOT - 1)

    loads = [
        pltpu.make_async_copy(w_hbm, work, local.at[0]),
        pltpu.make_async_copy(a_hbm, a_all.at[1], local.at[1]),
        pltpu.make_async_copy(b_hbm, b_all.at[1], local.at[2]),
    ]
    factor_loads = [
        pltpu.make_async_copy(ia_hbm.at[slot], ia, local.at[3]),
        pltpu.make_async_copy(vb_hbm, vb, local.at[4]),
        pltpu.make_async_copy(va_hbm.at[slot], va, local.at[5]),
        pltpu.make_async_copy(ib_hbm, ib, local.at[6]),
    ]
    loads[0].start()

    @pl.when(owner)
    def _():
        for load in factor_loads:
            load.start()

    loads[1].start()
    loads[2].start()

    barrier = pltpu.get_barrier_semaphore()
    friends = [at_column(rem(c + by, N_COL)) for by in (1, 31, 2, 30)]
    friends += [at_row(rem(r + by, 8)) for by in (1, 7)]
    friends += [place(zl=1 - zl), place(x=rem(x + 1, 4)), place(x=rem(x + 3, 4))]
    friends += [place(k=1 - k), place(y=rem(y + 1, 4)), place(y=rem(y + 3, 4))]
    friends += [place(zh=rem(zh + by, 4)) for by in (1, 2, 3)]
    for friend in friends:
        pl.semaphore_signal(barrier, inc=1, device_id=friend, device_id_type=MESH)

    @pl.when(owner)
    def _():
        left = jnp.concatenate(
            [la_ref[pl.ds(2 * slot, 1), :], la_ref[pl.ds(2 * slot + 1, 1), :]], axis=1
        )
        right = jnp.concatenate([lb_ref[pl.ds(0, 1), :], lb_ref[pl.ds(1, 1), :]], axis=1)
        denominator[...] = jnp.broadcast_to(left, (BLOCK, BLOCK)).T + right
        for load in factor_loads:
            load.wait()

    pl.semaphore_wait(barrier, len(friends))
    for load in loads:
        load.wait()

    def block_of(ref, *index):
        return jnp.concatenate(
            [ref[(*index, pl.ds(0, BLOCK, 2), slice(None))], ref[(*index, pl.ds(1, BLOCK, 2), slice(None))]],
            axis=1,
        )

    def put_work(q, value):
        work[q, pl.ds(0, BLOCK, 2), :] = value[:, :HALF]
        work[q, pl.ds(1, BLOCK, 2), :] = value[:, HALF:]

    def shift_copies(q):
        above = 8 * q + r < c
        up_slot = jnp.minimum(q + div(r, 7), N_SLOT - 1)
        first_row = jnp.where(r == 0, 1, 0)
        down_slot = jnp.maximum(q - first_row, 0)
        yield above, remote(
            a_hbm.at[q], a_all.at[0, q], a_send.at[0, q], a_recv.at[0, q], at_column(jnp.maximum(c - 1, 0))
        )
        yield above, remote(
            b_hbm.at[q], b_all.at[0, up_slot], b_send.at[0, q], b_recv.at[0, up_slot], at_row(rem(r + 1, 8))
        )
        yield above & (c + 1 < N_COL), remote(
            a_hbm.at[q], a_all.at[2, q], a_send.at[2, q], a_recv.at[2, q], at_column(jnp.minimum(c + 1, N_COL - 1))
        )
        yield above & (8 * q + r > 0), remote(
            b_hbm.at[q], b_all.at[2, down_slot], b_send.at[2, q], b_recv.at[2, down_slot], at_row(rem(r + 7, 8))
        )
        yield above & (c + 2 < N_COL) & (k == 0), remote(
            a_hbm.at[q], a_all.at[3, q], a_send.at[3, q], a_recv.at[3, q], at_column(jnp.minimum(c + 2, N_COL - 1))
        )

    def passed_copies(q):
        above = 8 * q + r + 1 < c
        first_row = jnp.where(r == 0, 1, 0)
        down_slot = jnp.maximum(q - first_row, 0)
        here = 8 * q + r < c - 1
        yield here, here & (k == 0), remote(
            a_all.at[2, q], a_all.at[3, q], a_send.at[1, q], a_recv.at[3, q], place(k=1 - k)
        ), remote(a_all.at[2, q], a_all.at[2, q], a_send.at[2, q], a_recv.at[2, q], place(k=1 - k))
        yield above, above & (8 * q + r > 0), remote(
            b_all.at[2, q], b_all.at[3, down_slot], b_send.at[3, q], b_recv.at[3, down_slot], at_row(rem(r + 7, 8))
        ), remote(b_all.at[2, q], b_all.at[2, q], b_send.at[2, q], b_recv.at[2, q], at_row(rem(r + 7, 8)))

    def column_role(f):
        i0 = c - f + 1
        exists = (i0 >= 0) & (i0 < N_COL)
        r0 = rem(i0 + 8, 8)
        dx = rem(x - rem(r0, 4) + 4, 4)
        same = zl == div(r0, 4)
        return exists, dx, same

    def column_copies(f, t):
        exists, dx, same = column_role(f)
        half = x_col.at[f, pl.ds(t * HALF, HALF), :]

        def to(n, where):
            return remote(half, half, col_send.at[f, t, n], col_recv.at[f, t], where)

        outer = 1 if t == 0 else 3
        yield exists & (dx == 0) & same, to(0, place(zl=1 - zl))
        if t == 0:
            yield exists & (dx <= 1), to(1, place(x=rem(x + 1, 4)))
            yield exists & (dx == 0), to(2, place(x=rem(x + 3, 4)))
        else:
            yield exists & (dx == 0), to(1, place(x=rem(x + 1, 4)))
            yield exists & ((dx == 0) | (dx == outer)), to(2, place(x=rem(x + 3, 4)))

    def column_arrival(f, t):
        exists, dx, same = column_role(f)
        half = x_col.at[f, pl.ds(t * HALF, HALF), :]
        source = (dx == 0) & same
        return exists & jnp.logical_not(source), remote(
            half, half, col_send.at[f, t, 0], col_recv.at[f, t], place(zl=1 - zl)
        )

    def row_role(f, q):
        total = r + f + 7
        place_in = rem(total, 8)
        plane = q + div(total, 8) - 1
        dy = rem(y - div(place_in, 2) + 4, 4)
        same = k == rem(place_in, 2)
        return plane, (plane >= 0) & (plane <= zh), dy, same

    def row_copies(f, q, t):
        plane, present, dy, same = row_role(f, q)
        half = x_row.at[f, q, pl.ds(t * HALF, HALF), :]

        def to(sem, where):
            return remote(half, half, sem, row_recv.at[f, q, t], where)

        carrier = present & same
        yield carrier, to(row_send.at[f, q, t, 0], place(k=1 - k))
        first, last = (dy <= 1, dy == 0) if t == 0 else (dy == 0, (dy == 0) | (dy == 3))
        yield carrier & first, to(row_send.at[f, q, t, 1], place(y=rem(y + 1, 4)))
        yield carrier & last, to(row_send.at[f, q, t, 2], place(y=rem(y + 3, 4)))

    def far_copies(f, q, t):
        half = x_row.at[f, q, pl.ds(t * HALF, HALF), :]
        for by in (1, 2, 3):
            yield zh + by < 4, remote(
                half, half, row_far.at[t, by - 1], row_recv.at[f, q, t], place(zh=jnp.minimum(zh + by, 3))
            )

    def row_arrival(f, q, t):
        plane, present, dy, same = row_role(f, q)
        half = x_row.at[f, q, pl.ds(t * HALF, HALF), :]
        source = (plane == zh) & (dy == 0) & same
        return present & jnp.logical_not(source), remote(
            half, half, row_send.at[f, q, t, 0], row_recv.at[f, q, t], place(k=1 - k)
        )

    def start(condition, copy):
        @pl.when(condition)
        def _():
            copy.start()

    def drain(condition, copy):
        @pl.when(condition)
        def _():
            copy.wait_send()

    def land(condition, copy):
        @pl.when(condition)
        def _():
            copy.wait_recv()

    def update(f, q):
        upper = c - f + 1 < N_COL
        lower = 8 * q + r + f - 1 >= 0
        early = (f == 0) | (f == 3)
        land(upper & early, remote(a_all.at[f, q], a_all.at[f, q], a_send.at[f, q], a_recv.at[f, q], place(k=1 - k)))
        land(lower & early, remote(b_all.at[f, q], b_all.at[f, q], b_send.at[f, q], b_recv.at[f, q], place(k=1 - k)))

        @pl.when(upper)
        def _():
            put_work(q, block_of(work, q) - matmul(block_of(a_all, f, q), x_col[f]))

        @pl.when(lower)
        def _():
            put_work(q, block_of(work, q) - matmul(x_row[f, q], block_of(b_all, f, q)))

    def bulk(f):
        def one(q, carry):
            done_before = owner & (q == own_slot)

            @pl.when((c - 8 * q - r >= f) & jnp.logical_not(done_before))
            def _():
                update(f, q)

            return carry

        lax.fori_loop(0, N_SLOT, one, 0)

    def front(f, carry):
        @pl.when(owner & (own_front == f))
        def _():
            rotated = matmul(matmul(ia[...], block_of(work, slot)), vb[...])
            solved = matmul(matmul(va[...], rotated / denominator[...]), ib[...])
            x_col[f] = solved
            x_row[f, slot] = solved
            put_work(slot, solved)
            for t in (0, 1):
                for condition, copy in column_copies(f, t):
                    start(condition, copy)
                for condition, copy in row_copies(f, slot, t):
                    start(condition, copy)
            for t in (0, 1):
                for condition, copy in far_copies(f, slot, t):
                    start(condition, copy)

        @pl.when(f == 0)
        def _():
            def one(step, carry):
                for condition, copy in shift_copies(N_SLOT - 1 - step):
                    start(condition, copy)
                return carry

            lax.fori_loop(0, N_SLOT, one, 0)

        @pl.when(f > 0)
        def _():
            bulk(f - 1)

        for t in (0, 1):
            arriving, arrival = column_arrival(f, t)

            @pl.when(arriving)
            def _():
                arrival.wait_recv()
                for condition, copy in column_copies(f, t):
                    start(condition, copy)

        def hand_on(step, carry):
            q = N_SLOT - 1 - step
            for t in (0, 1):
                arriving, arrival = row_arrival(f, q, t)

                @pl.when(arriving)
                def _():
                    arrival.wait_recv()
                    for condition, copy in row_copies(f, q, t):
                        start(condition, copy)

            return carry

        lax.fori_loop(0, N_SLOT, hand_on, 0)

        @pl.when(owner & (f < own_front))
        def _():
            update(f, slot)

        @pl.when(f == 1)
        def _():
            def one(step, carry):
                for arrived, forwarded, copy, arrival in passed_copies(N_SLOT - 1 - step):
                    land(arrived, arrival)
                    start(forwarded, copy)
                return carry

            lax.fori_loop(0, N_SLOT, one, 0)

        return carry

    lax.fori_loop(0, FRONTS, front, 0)
    bulk(FRONTS - 1)

    result = pltpu.make_async_copy(work, out_hbm, out_sem)
    result.start()

    def finish(q, carry):
        for condition, copy in shift_copies(q):
            drain(condition, copy)
        for _, forwarded, copy, _ in passed_copies(q):
            drain(forwarded, copy)
        return carry

    lax.fori_loop(0, N_SLOT, finish, 0)

    def finish_front(f, carry):
        for t in (0, 1):
            for condition, copy in column_copies(f, t):
                drain(condition, copy)

        def one(q, carry):
            for t in (0, 1):
                for condition, copy in row_copies(f, q, t):
                    drain(condition, copy)
            return carry

        return lax.fori_loop(0, N_SLOT, one, carry)

    lax.fori_loop(0, FRONTS, finish_front, 0)

    @pl.when(owner)
    def _():
        for t in (0, 1):
            for condition, copy in far_copies(own_front, slot, t):
                drain(condition, copy)

    result.wait()


def body(
    upper_a, upper_b, right_side, vectors_a, inverse_a, values_a, vectors_b, inverse_b, values_b
):
    tall = (N_SLOT, 2 * BLOCK, HALF)
    square = (N_SLOT, BLOCK, BLOCK)
    anywhere = pl.BlockSpec(memory_space=pl.ANY)
    inside = pl.BlockSpec(memory_space=pltpu.VMEM)
    dma = pltpu.SemaphoreType.DMA
    solved = pl.pallas_call(
        kernel,
        out_shape=jax.ShapeDtypeStruct(tall, jnp.float32),
        in_specs=[anywhere] * 5 + [inside] + [anywhere] * 2 + [inside],
        out_specs=anywhere,
        scratch_shapes=[
            pltpu.VMEM((FRONTS, *tall), jnp.float32),
            pltpu.VMEM((FRONTS, *tall), jnp.float32),
            pltpu.VMEM(tall, jnp.float32),
            pltpu.VMEM(square, jnp.float32),
            pltpu.VMEM((FRONTS, *square), jnp.float32),
            *[pltpu.VMEM((BLOCK, BLOCK), jnp.float32)] * 5,
            dma((4, N_SLOT)),
            dma((4, N_SLOT)),
            dma((4, N_SLOT)),
            dma((4, N_SLOT)),
            dma((FRONTS, N_SLOT, 2, 3)),
            dma((2, 3)),
            dma((FRONTS, N_SLOT, 2)),
            dma((FRONTS, 2, 3)),
            dma((FRONTS, 2)),
            dma((7,)),
            dma,
        ],
        compiler_params=pltpu.CompilerParams(
            collective_id=0, has_side_effects=True, vmem_limit_bytes=48 * 1024 * 1024
        ),
    )(
        upper_a.reshape(tall), upper_b.reshape(tall), right_side.reshape(tall),
        vectors_a.reshape(square), inverse_a.reshape(square), values_a.reshape(2 * N_SLOT, HALF),
        vectors_b.reshape(BLOCK, BLOCK), inverse_b.reshape(BLOCK, BLOCK), values_b.reshape(2, HALF),
    )
    return solved.reshape(right_side.shape)


def solution(mesh):
    finer = Mesh(mesh.devices.reshape(2, 4, 4, 4, 2), ROW + COL)
    whole = P(None, ROW, None, COL, None)
    placed = (
        whole, whole, whole,
        P(None, ROW, None, None), P(None, ROW, None, None), P(None, ROW, None),
        P(COL, None, None), P(COL, None, None), P(COL, None),
    )
    return jax.shard_map(body, mesh=finer, in_specs=placed, out_specs=whole, check_vma=False)
```

time: 439 us -> 148 us (0.34)
  the two profiles are of different devices: /device:TPU:192 before, /device:TPU:245 now
where the time goes in v1:
time: 148 us
  Pallas kernels  140 us (95%)
  local copies, waits for them, and re-layouts  8.46 us (6%)
    pallas_call x1, Pallas kernels, body(): pl.pallas_call(kernel, out_shape=jax.ShapeDtypeStruct(tall, jnp.float32),...  140 us
    unnamed x17, local copies, waits for them, and re-layouts  8.46 us

profile of v1, /device:TPU:245, one launch (start us, length us, event | category | flops | bytes accessed | tf_op | source)
XLA Modules:
  0.0 148.0 jit_solution(112469984217333342)
XLA Ops:
  0.0 0.0 copy-start.6
  0.0 0.0 copy-start.7
  0.0 0.7 copy-done.6
  0.7 0.0 copy-done.7
  0.7 0.0 copy-start
  0.7 1.2 copy-done
  1.9 0.0 copy-start.1
  1.9 1.2 copy-done.1
  3.1 0.0 copy-start.2
  3.1 1.2 copy-done.2
  4.4 0.0 copy-start.3
  4.4 1.2 copy-done.3
  5.6 0.0 copy-start.4
  5.6 0.9 copy-done.4
  6.5 0.0 copy-start.5
  6.5 0.9 copy-done.5
  7.5 139.6 %shard_map.91 = f32[4,512,128]{2,1,0:T(8,128)S(1)} custom-call(f32[4,512,128]{2,1,0:T(8,128)S(1)} %bitcast.11, f32[4,512,128]{2,1,0:T(8,128)S(1)} %bitcast.12, f32[4,512,128]{2,1,0:T(8,128)S(1)} %bitcast.13, f32[4,256,256]{2,1,0:T(8,128)S(1)} %bitcast.14, f32[4,256,256]{2,1,0:T(8,128)} %bitcast.19, f32[8,128]{1,0:T(8,128)S(1)} %bitcast.17, ...), custom_call_target="tpu_custom_call" | custom-call | tf_op jit(solution)/shard_map/pallas_call | solution.py:380
  147.1 1.0 copy.12
Async XLA Ops:
  0.0 0.7 copy-start.6
  0.0 0.7 copy-start.7
  0.7 1.2 copy-start
  1.9 1.2 copy-start.1
  3.1 1.2 copy-start.2
  4.4 1.2 copy-start.3
  5.6 0.9 copy-start.4
  6.5 0.9 copy-start.5

commit v2 on v1

--- a/solution.py
+++ b/solution.py
@@ -34,8 +34,8 @@
 
 def kernel(
     a_hbm, b_hbm, w_hbm, va_hbm, ia_hbm, la_ref, vb_hbm, ib_hbm, lb_ref, out_hbm,
-    a_all, b_all, work, x_col, x_row, va, ia, vb, ib, denominator,
-    a_send, a_recv, b_send, b_recv, row_send, row_far, row_recv, col_send, col_recv, local, out_sem,
+    a_all, b_all, work, x_col, x_row, chain_col, chain_row, va, ia, vb, ib, denominator,
+    a_send, a_recv, b_send, b_recv, row_send, row_far, row_recv, col_send, col_recv, chain_send, chain_recv, local, out_sem,
 ):
     zl, x = lax.axis_index("zl"), lax.axis_index("x")
     zh, y, k = lax.axis_index("zh"), lax.axis_index("y"), lax.axis_index("k")
@@ -85,10 +85,9 @@
     loads[2].start()
 
     barrier = pltpu.get_barrier_semaphore()
-    friends = [at_column(rem(c + by, N_COL)) for by in (1, 31, 2, 30)]
-    friends += [at_row(rem(r + by, 8)) for by in (1, 7)]
-    friends += [place(zl=1 - zl), place(x=rem(x + 1, 4)), place(x=rem(x + 3, 4))]
-    friends += [place(k=1 - k), place(y=rem(y + 1, 4)), place(y=rem(y + 3, 4))]
+    friends = [at_column(rem(c + by, N_COL)) for by in (1, 31, 2, 30, 3, 29)]
+    friends += [at_row(rem(r + by, 8)) for by in range(1, 8)]
+    friends += [place(k=1 - k)] + [place(y=rem(y + by, 4)) for by in (1, 2, 3)]
     friends += [place(zh=rem(zh + by, 4)) for by in (1, 2, 3)]
     for friend in friends:
         pl.semaphore_signal(barrier, inc=1, device_id=friend, device_id_type=MESH)
@@ -103,9 +102,11 @@
         for load in factor_loads:
             load.wait()
 
-    pl.semaphore_wait(barrier, len(friends))
-    for load in loads:
-        load.wait()
+    with jax.named_scope("barrier"):
+        pl.semaphore_wait(barrier, len(friends))
+    with jax.named_scope("loads"):
+        for load in loads:
+            load.wait()
 
     def block_of(ref, *index):
         return jnp.concatenate(
@@ -117,36 +118,44 @@
         work[q, pl.ds(0, BLOCK, 2), :] = value[:, :HALF]
         work[q, pl.ds(1, BLOCK, 2), :] = value[:, HALF:]
 
+    near_slot = div(c - 1 - r + 8, 8) - 1
+
     def shift_copies(q):
         above = 8 * q + r < c
+        near = q == near_slot
         up_slot = jnp.minimum(q + div(r, 7), N_SLOT - 1)
-        first_row = jnp.where(r == 0, 1, 0)
-        down_slot = jnp.maximum(q - first_row, 0)
-        yield above, remote(
+        down_slot = jnp.maximum(q - jnp.where(r == 0, 1, 0), 0)
+        yield True, above, remote(
             a_hbm.at[q], a_all.at[0, q], a_send.at[0, q], a_recv.at[0, q], at_column(jnp.maximum(c - 1, 0))
         )
-        yield above, remote(
+        yield True, above, remote(
             b_hbm.at[q], b_all.at[0, up_slot], b_send.at[0, q], b_recv.at[0, up_slot], at_row(rem(r + 1, 8))
         )
-        yield above & (c + 1 < N_COL), remote(
+        to_right = above & (c + 1 < N_COL)
+        to_above = above & (8 * q + r > 0)
+        right = remote(
             a_hbm.at[q], a_all.at[2, q], a_send.at[2, q], a_recv.at[2, q], at_column(jnp.minimum(c + 1, N_COL - 1))
         )
-        yield above & (8 * q + r > 0), remote(
+        higher = remote(
             b_hbm.at[q], b_all.at[2, down_slot], b_send.at[2, q], b_recv.at[2, down_slot], at_row(rem(r + 7, 8))
         )
-        yield above & (c + 2 < N_COL) & (k == 0), remote(
+        yield True, to_right & near, right
+        yield True, to_above & near, higher
+        yield False, to_right & jnp.logical_not(near), right
+        yield False, to_above & jnp.logical_not(near), higher
+        yield False, above & (c + 2 < N_COL) & (k == 0), remote(
             a_hbm.at[q], a_all.at[3, q], a_send.at[3, q], a_recv.at[3, q], at_column(jnp.minimum(c + 2, N_COL - 1))
         )
 
     def passed_copies(q):
         above = 8 * q + r + 1 < c
-        first_row = jnp.where(r == 0, 1, 0)
-        down_slot = jnp.maximum(q - first_row, 0)
+        down_slot = jnp.maximum(q - jnp.where(r == 0, 1, 0), 0)
+        fresh = jnp.logical_not(owner & (own_front == 3) & (q == own_slot))
         here = 8 * q + r < c - 1
-        yield here, here & (k == 0), remote(
+        yield here & fresh, here & (k == 0), remote(
             a_all.at[2, q], a_all.at[3, q], a_send.at[1, q], a_recv.at[3, q], place(k=1 - k)
         ), remote(a_all.at[2, q], a_all.at[2, q], a_send.at[2, q], a_recv.at[2, q], place(k=1 - k))
-        yield above, above & (8 * q + r > 0), remote(
+        yield above & fresh, above & (8 * q + r > 0), remote(
             b_all.at[2, q], b_all.at[3, down_slot], b_send.at[3, q], b_recv.at[3, down_slot], at_row(rem(r + 7, 8))
         ), remote(b_all.at[2, q], b_all.at[2, q], b_send.at[2, q], b_recv.at[2, q], at_row(rem(r + 7, 8)))
 
@@ -165,14 +174,13 @@
         def to(n, where):
             return remote(half, half, col_send.at[f, t, n], col_recv.at[f, t], where)
 
-        outer = 1 if t == 0 else 3
-        yield exists & (dx == 0) & same, to(0, place(zl=1 - zl))
-        if t == 0:
-            yield exists & (dx <= 1), to(1, place(x=rem(x + 1, 4)))
-            yield exists & (dx == 0), to(2, place(x=rem(x + 3, 4)))
-        else:
-            yield exists & (dx == 0), to(1, place(x=rem(x + 1, 4)))
-            yield exists & ((dx == 0) | (dx == outer)), to(2, place(x=rem(x + 3, 4)))
+        source = exists & (dx == 0) & same
+        twin = exists & (dx == 0) & jnp.logical_not(same) & (f < FRONTS - 1)
+        yield source, to(3, place(zl=1 - zl))
+        for by in (3, 1, 2):
+            yield source | twin, to(by - 1, place(x=rem(x + by, 4)))
+        for by in (3, 1, 2):
+            yield source & (f == FRONTS - 1), to(3 + by, place(zl=1 - zl, x=rem(x + by, 4)))
 
     def column_arrival(f, t):
         exists, dx, same = column_role(f)
@@ -199,9 +207,10 @@
 
         carrier = present & same
         yield carrier, to(row_send.at[f, q, t, 0], place(k=1 - k))
-        first, last = (dy <= 1, dy == 0) if t == 0 else (dy == 0, (dy == 0) | (dy == 3))
-        yield carrier & first, to(row_send.at[f, q, t, 1], place(y=rem(y + 1, 4)))
-        yield carrier & last, to(row_send.at[f, q, t, 2], place(y=rem(y + 3, 4)))
+        if t == 0:
+            yield carrier & (dy != 3), to(row_send.at[f, q, t, 1], place(y=rem(y + 1, 4)))
+        else:
+            yield carrier & (dy != 1), to(row_send.at[f, q, t, 1], place(y=rem(y + 3, 4)))
 
     def far_copies(f, q, t):
         half = x_row.at[f, q, pl.ds(t * HALF, HALF), :]
@@ -233,20 +242,24 @@
         def _():
             copy.wait_recv()
 
+    def subtract_upper(f, q, arrived, solved):
+        land(arrived, remote(a_all.at[f, q], a_all.at[f, q], a_send.at[f, q], a_recv.at[f, q], place(k=1 - k)))
+        put_work(q, block_of(work, q) - matmul(block_of(a_all, f, q), solved))
+
+    def subtract_lower(f, q, arrived, solved):
+        land(arrived, remote(b_all.at[f, q], b_all.at[f, q], b_send.at[f, q], b_recv.at[f, q], place(k=1 - k)))
+        put_work(q, block_of(work, q) - matmul(solved, block_of(b_all, f, q)))
+
     def update(f, q):
-        upper = c - f + 1 < N_COL
-        lower = 8 * q + r + f - 1 >= 0
         early = (f == 0) | (f == 3)
-        land(upper & early, remote(a_all.at[f, q], a_all.at[f, q], a_send.at[f, q], a_recv.at[f, q], place(k=1 - k)))
-        land(lower & early, remote(b_all.at[f, q], b_all.at[f, q], b_send.at[f, q], b_recv.at[f, q], place(k=1 - k)))
-
-        @pl.when(upper)
-        def _():
-            put_work(q, block_of(work, q) - matmul(block_of(a_all, f, q), x_col[f]))
-
-        @pl.when(lower)
-        def _():
-            put_work(q, block_of(work, q) - matmul(x_row[f, q], block_of(b_all, f, q)))
+
+        @pl.when(c - f + 1 < N_COL)
+        def _():
+            subtract_upper(f, q, early, x_col[f])
+
+        @pl.when(8 * q + r + f - 1 >= 0)
+        def _():
+            subtract_lower(f, q, early, x_row[f, q])
 
     def bulk(f):
         def one(q, carry):
@@ -260,90 +273,164 @@
 
         lax.fori_loop(0, N_SLOT, one, 0)
 
-    def front(f, carry):
-        @pl.when(owner & (own_front == f))
-        def _():
+    def chain_copies(distances):
+        i0 = 8 * own_slot + r
+        for by in distances:
+            later = own_front + by < FRONTS
+            f = jnp.minimum(own_front, 2)
+            yield later & (c + by < N_COL), remote(
+                x_row.at[own_front, slot], chain_row.at[f], chain_send.at[0, by - 1], chain_recv.at[0, f],
+                at_column(jnp.minimum(c + by, N_COL - 1)),
+            )
+            yield later & (i0 - by >= 0), remote(
+                x_col.at[own_front], chain_col.at[f], chain_send.at[1, by - 1], chain_recv.at[1, f],
+                at_row(rem(r + 8 - by, 8)),
+            )
+
+    def send_shifts(wanted):
+        def one(step, carry):
+            for first, condition, copy in shift_copies(N_SLOT - 1 - step):
+                if first == wanted:
+                    start(condition, copy)
+            return carry
+
+        lax.fori_loop(0, N_SLOT, one, 0)
+
+    deferred = owner & (own_front < 2)
+    send_shifts(True)
+
+    @pl.when(jnp.logical_not(deferred))
+    def _():
+        send_shifts(False)
+
+    @pl.when(owner)
+    def _():
+        def earlier(f, carry):
+            @pl.when((f < own_front) & (c - f + 1 < N_COL))
+            def _():
+                with jax.named_scope("chain_col"):
+                    land(True, remote(chain_col.at[f], chain_col.at[f], chain_send.at[1, 0], chain_recv.at[1, f], place(k=1 - k)))
+                with jax.named_scope("chain_upper"):
+                    subtract_upper(f, slot, f != 1, chain_col[f])
+
+            @pl.when((f < own_front) & (8 * slot + r + f - 1 >= 0))
+            def _():
+                with jax.named_scope("chain_row"):
+                    land(True, remote(chain_row.at[f], chain_row.at[f], chain_send.at[0, 0], chain_recv.at[0, f], place(k=1 - k)))
+                with jax.named_scope("chain_lower"):
+                    subtract_lower(f, slot, f != 1, chain_row[f])
+
+            return carry
+
+        lax.fori_loop(0, FRONTS - 1, earlier, 0)
+        with jax.named_scope("solve"):
             rotated = matmul(matmul(ia[...], block_of(work, slot)), vb[...])
             solved = matmul(matmul(va[...], rotated / denominator[...]), ib[...])
-            x_col[f] = solved
-            x_row[f, slot] = solved
+            x_col[own_front] = solved
+            x_row[own_front, slot] = solved
             put_work(slot, solved)
-            for t in (0, 1):
+        for condition, copy in chain_copies((1,)):
+            start(condition, copy)
+        for t in (0, 1):
+            for condition, copy in far_copies(own_front, slot, t):
+                start(condition, copy)
+        for t in (0, 1):
+            for condition, copy in column_copies(own_front, t):
+                start(condition, copy)
+            for condition, copy in row_copies(own_front, slot, t):
+                start(condition, copy)
+        for condition, copy in chain_copies((2, 3)):
+            start(condition, copy)
+
+    @pl.when(deferred)
+    def _():
+        send_shifts(False)
+
+    def receive_column(f):
+        for t in (0, 1):
+            arriving, arrival = column_arrival(f, t)
+
+            @pl.when(arriving)
+            def _():
+                with jax.named_scope(f"col#t={t}"):
+                    arrival.wait_recv()
                 for condition, copy in column_copies(f, t):
                     start(condition, copy)
-                for condition, copy in row_copies(f, slot, t):
-                    start(condition, copy)
+
+    distance = rem(c - r + 32, 8)
+    relays_column = (distance >= 3) & (distance <= 5)
+
+    @pl.when(relays_column)
+    def _():
+        receive_column(jnp.clip(distance - 3, 0, FRONTS - 1))
+
+    mine = rem(k + r + 1, 2)
+
+    def receive_row(f, q, t, wanted):
+        arriving, arrival = row_arrival(f, q, t)
+
+        @pl.when(arriving & wanted)
+        def _():
+            with jax.named_scope(f"row#t={t}"):
+                arrival.wait_recv()
+            for condition, copy in row_copies(f, q, t):
+                start(condition, copy)
+
+    def pass_on(step, carry):
+        for arrived, forwarded, copy, arrival in passed_copies(N_SLOT - 1 - step):
+            land(arrived, arrival)
+            start(forwarded, copy)
+        return carry
+
+    def ring(n, carry):
+        def one(step, carry):
+            f = mine + 2 * div(step, N_SLOT)
+            q = N_SLOT - 1 - rem(step, N_SLOT)
+            _, _, dy, _ = row_role(f, q)
+            receive_row(f, q, 0, dy == n)
+            receive_row(f, q, 1, rem(4 - dy, 4) == n)
+            return carry
+
+        lax.fori_loop(0, 2 * N_SLOT, one, 0)
+
+        @pl.when(n == 1)
+        def _():
+            with jax.named_scope("pass"):
+                lax.fori_loop(0, N_SLOT, pass_on, 0)
+
+        return carry
+
+    lax.fori_loop(0, 4, ring, 0)
+
+    def front(f, carry):
+        @pl.when(jnp.logical_not(relays_column & (f == distance - 3)))
+        def _():
+            receive_column(f)
+
+        def one(q, carry):
             for t in (0, 1):
-                for condition, copy in far_copies(f, slot, t):
-                    start(condition, copy)
-
-        @pl.when(f == 0)
-        def _():
-            def one(step, carry):
-                for condition, copy in shift_copies(N_SLOT - 1 - step):
-                    start(condition, copy)
-                return carry
-
-            lax.fori_loop(0, N_SLOT, one, 0)
-
-        @pl.when(f > 0)
-        def _():
-            bulk(f - 1)
-
-        for t in (0, 1):
-            arriving, arrival = column_arrival(f, t)
-
-            @pl.when(arriving)
-            def _():
-                arrival.wait_recv()
-                for condition, copy in column_copies(f, t):
-                    start(condition, copy)
-
-        def hand_on(step, carry):
-            q = N_SLOT - 1 - step
-            for t in (0, 1):
-                arriving, arrival = row_arrival(f, q, t)
-
-                @pl.when(arriving)
-                def _():
-                    arrival.wait_recv()
-                    for condition, copy in row_copies(f, q, t):
-                        start(condition, copy)
-
+                receive_row(f, q, t, rem(f, 2) != mine)
             return carry
 
-        lax.fori_loop(0, N_SLOT, hand_on, 0)
-
-        @pl.when(owner & (f < own_front))
-        def _():
-            update(f, slot)
-
-        @pl.when(f == 1)
-        def _():
-            def one(step, carry):
-                for arrived, forwarded, copy, arrival in passed_copies(N_SLOT - 1 - step):
-                    land(arrived, arrival)
-                    start(forwarded, copy)
-                return carry
-
-            lax.fori_loop(0, N_SLOT, one, 0)
-
+        lax.fori_loop(0, N_SLOT, one, 0)
+        with jax.named_scope("bulk"):
+            bulk(f)
         return carry
 
     lax.fori_loop(0, FRONTS, front, 0)
-    bulk(FRONTS - 1)
 
     result = pltpu.make_async_copy(work, out_hbm, out_sem)
     result.start()
 
     def finish(q, carry):
-        for condition, copy in shift_copies(q):
+        for _, condition, copy in shift_copies(q):
             drain(condition, copy)
         for _, forwarded, copy, _ in passed_copies(q):
             drain(forwarded, copy)
         return carry
 
-    lax.fori_loop(0, N_SLOT, finish, 0)
+    with jax.named_scope("finish"):
+        lax.fori_loop(0, N_SLOT, finish, 0)
 
     def finish_front(f, carry):
         for t in (0, 1):
@@ -358,10 +445,13 @@
 
         return lax.fori_loop(0, N_SLOT, one, carry)
 
-    lax.fori_loop(0, FRONTS, finish_front, 0)
+    with jax.named_scope("finish_front"):
+        lax.fori_loop(0, FRONTS, finish_front, 0)
 
     @pl.when(owner)
     def _():
+        for condition, copy in chain_copies((1, 2, 3)):
+            drain(condition, copy)
         for t in (0, 1):
             for condition, copy in far_copies(own_front, slot, t):
                 drain(condition, copy)
@@ -388,21 +478,24 @@
             pltpu.VMEM(tall, jnp.float32),
             pltpu.VMEM(square, jnp.float32),
             pltpu.VMEM((FRONTS, *square), jnp.float32),
+            *[pltpu.VMEM((FRONTS - 1, BLOCK, BLOCK), jnp.float32)] * 2,
             *[pltpu.VMEM((BLOCK, BLOCK), jnp.float32)] * 5,
             dma((4, N_SLOT)),
             dma((4, N_SLOT)),
             dma((4, N_SLOT)),
             dma((4, N_SLOT)),
-            dma((FRONTS, N_SLOT, 2, 3)),
+            dma((FRONTS, N_SLOT, 2, 2)),
             dma((2, 3)),
             dma((FRONTS, N_SLOT, 2)),
-            dma((FRONTS, 2, 3)),
+            dma((FRONTS, 2, 7)),
             dma((FRONTS, 2)),
+            dma((2, 3)),
+            dma((2, 3)),
             dma((7,)),
             dma,
         ],
         compiler_params=pltpu.CompilerParams(
-            collective_id=0, has_side_effects=True, vmem_limit_bytes=48 * 1024 * 1024
+            collective_id=0, has_side_effects=True, vmem_limit_bytes=60 * 1024 * 1024
         ),
     )(
         upper_a.reshape(tall), upper_b.reshape(tall), right_side.reshape(tall),

time: 148 us -> 115 us (0.78)
  the two profiles are of different devices: /device:TPU:245 before, /device:TPU:229 now
where the time goes in v2:
time: 115 us
  Pallas kernels  112 us (97%)
  local copies, waits for them, and re-layouts  2.91 us (3%)
    pallas_call x1, Pallas kernels, body(): pl.pallas_call(kernel, out_shape=jax.ShapeDtypeStruct(tall, jnp.float32),...  112 us
    unnamed x1, local copies, waits for them, and re-layouts  2.91 us

profile of v2, /device:TPU:229, one launch (start us, length us, event | category | flops | bytes accessed | tf_op | source)
XLA Modules:
  0.0 114.6 jit_solution(17903512168117981077)
XLA Ops:
  0.0 111.7 %shard_map.91 = f32[4,512,128]{2,1,0:T(8,128)} custom-call(f32[4,512,128]{2,1,0:T(8,128)} %bitcast.11, f32[4,512,128]{2,1,0:T(8,128)} %bitcast.12, f32[4,512,128]{2,1,0:T(8,128)} %bitcast.13, f32[4,256,256]{2,1,0:T(8,128)} %bitcast.14, f32[4,256,256]{2,1,0:T(8,128)} %bitcast.15, f32[8,128]{1,0:T(8,128)} %bitcast.18, f32[256,256]{1,0:T(8,128)} %bitcast.16, ...), custom_call_target="tpu_custom_call" | custom-call | tf_op jit(solution)/shard_map/pallas_call | solution.py:470
  111.7 2.9 %copy.12 = f32[4,1,256,1,256]{4,3,2,1,0:T(1,128)} copy(f32[4,1,256,1,256]{4,3,2,1,0:T(1,128)} %bitcast.10) | data formatting | bytes 2097152

commit v3 on v2

--- a/solution.py
+++ b/solution.py
@@ -85,7 +85,7 @@
     loads[2].start()
 
     barrier = pltpu.get_barrier_semaphore()
-    friends = [at_column(rem(c + by, N_COL)) for by in (1, 31, 2, 30, 3, 29)]
+    friends = [at_column(rem(c + by, N_COL)) for by in (1, 31, 2, 30)]
     friends += [at_row(rem(r + by, 8)) for by in range(1, 8)]
     friends += [place(k=1 - k)] + [place(y=rem(y + by, 4)) for by in (1, 2, 3)]
     friends += [place(zh=rem(zh + by, 4)) for by in (1, 2, 3)]
@@ -118,46 +118,53 @@
         work[q, pl.ds(0, BLOCK, 2), :] = value[:, :HALF]
         work[q, pl.ds(1, BLOCK, 2), :] = value[:, HALF:]
 
+    distance = rem(c - r + 32, 8)
     near_slot = div(c - 1 - r + 8, 8) - 1
 
     def shift_copies(q):
         above = 8 * q + r < c
-        near = q == near_slot
-        up_slot = jnp.minimum(q + div(r, 7), N_SLOT - 1)
-        down_slot = jnp.maximum(q - jnp.where(r == 0, 1, 0), 0)
-        yield True, above, remote(
-            a_hbm.at[q], a_all.at[0, q], a_send.at[0, q], a_recv.at[0, q], at_column(jnp.maximum(c - 1, 0))
-        )
-        yield True, above, remote(
-            b_hbm.at[q], b_all.at[0, up_slot], b_send.at[0, q], b_recv.at[0, up_slot], at_row(rem(r + 1, 8))
-        )
-        to_right = above & (c + 1 < N_COL)
-        to_above = above & (8 * q + r > 0)
-        right = remote(
-            a_hbm.at[q], a_all.at[2, q], a_send.at[2, q], a_recv.at[2, q], at_column(jnp.minimum(c + 1, N_COL - 1))
-        )
-        higher = remote(
-            b_hbm.at[q], b_all.at[2, down_slot], b_send.at[2, q], b_recv.at[2, down_slot], at_row(rem(r + 7, 8))
-        )
-        yield True, to_right & near, right
-        yield True, to_above & near, higher
-        yield False, to_right & jnp.logical_not(near), right
-        yield False, to_above & jnp.logical_not(near), higher
-        yield False, above & (c + 2 < N_COL) & (k == 0), remote(
-            a_hbm.at[q], a_all.at[3, q], a_send.at[3, q], a_recv.at[3, q], at_column(jnp.minimum(c + 2, N_COL - 1))
-        )
-
-    def passed_copies(q):
-        above = 8 * q + r + 1 < c
-        down_slot = jnp.maximum(q - jnp.where(r == 0, 1, 0), 0)
+        near = (q == near_slot) & (distance >= 1) & (distance <= 3)
+        nearer = near & (distance == 1)
+        crossing = (rem(c, 8) >= 6) & (x != 1)
+        first_row = jnp.where(r == 0, 1, 0)
+        second_row = jnp.where(r <= 1, 1, 0)
+        left = at_column(jnp.maximum(c - 1, 0))
+        right = at_column(jnp.minimum(c + 1, N_COL - 1))
+        farther = at_column(jnp.minimum(c + 2, N_COL - 1))
+        below, higher, highest = at_row(rem(r + 1, 8)), at_row(rem(r + 7, 8)), at_row(rem(r + 6, 8))
+
+        def a_copy(f, where):
+            return remote(a_hbm.at[q], a_all.at[f, q], a_send.at[f, q], a_recv.at[f, q], where)
+
+        def b_copy(f, there, where):
+            target = jnp.clip(there, 0, N_SLOT - 1)
+            return remote(b_hbm.at[q], b_all.at[f, target], b_send.at[f, q], b_recv.at[f, target], where)
+
+        sends = [
+            (above, near, None, a_copy(0, left)),
+            (above, near, None, b_copy(0, q + div(r, 7), below)),
+            (above & (c + 1 < N_COL), nearer, crossing & (k == 1), a_copy(2, right)),
+            (above & (8 * q + r >= 1), nearer, None, b_copy(2, q - first_row, higher)),
+        ]
+        for number, (wanted, soon, later, copy) in enumerate(sends):
+            yield 0, wanted & soon, copy
+            rest = wanted & jnp.logical_not(soon)
+            if later is None:
+                yield 4 if number < 2 else 1, rest, copy
+            else:
+                yield 1, rest & jnp.logical_not(later), copy
+                yield 2, rest & later, copy
+        wanted = above & (c + 2 < N_COL) & (k == 0)
+        yield 1, wanted & jnp.logical_not(crossing), a_copy(3, farther)
+        yield 2, wanted & crossing, a_copy(3, farther)
+        yield 3, above & (8 * q + r >= 2), b_copy(3, q - second_row, highest)
+
+    def passed_copy(q):
         fresh = jnp.logical_not(owner & (own_front == 3) & (q == own_slot))
         here = 8 * q + r < c - 1
-        yield here & fresh, here & (k == 0), remote(
+        return here & fresh, here & (k == 0), remote(
             a_all.at[2, q], a_all.at[3, q], a_send.at[1, q], a_recv.at[3, q], place(k=1 - k)
         ), remote(a_all.at[2, q], a_all.at[2, q], a_send.at[2, q], a_recv.at[2, q], place(k=1 - k))
-        yield above & fresh, above & (8 * q + r > 0), remote(
-            b_all.at[2, q], b_all.at[3, down_slot], b_send.at[3, q], b_recv.at[3, down_slot], at_row(rem(r + 7, 8))
-        ), remote(b_all.at[2, q], b_all.at[2, q], b_send.at[2, q], b_recv.at[2, q], at_row(rem(r + 7, 8)))
 
     def column_role(f):
         i0 = c - f + 1
@@ -172,22 +179,22 @@
         half = x_col.at[f, pl.ds(t * HALF, HALF), :]
 
         def to(n, where):
-            return remote(half, half, col_send.at[f, t, n], col_recv.at[f, t], where)
+            return remote(half, half, col_send.at[t, n], col_recv.at[f, t], where)
 
         source = exists & (dx == 0) & same
-        twin = exists & (dx == 0) & jnp.logical_not(same) & (f < FRONTS - 1)
+        twin = exists & (dx == 0) & jnp.logical_not(same) & (f < 2)
         yield source, to(3, place(zl=1 - zl))
         for by in (3, 1, 2):
             yield source | twin, to(by - 1, place(x=rem(x + by, 4)))
         for by in (3, 1, 2):
-            yield source & (f == FRONTS - 1), to(3 + by, place(zl=1 - zl, x=rem(x + by, 4)))
+            yield source & (f >= 2), to(3 + by, place(zl=1 - zl, x=rem(x + by, 4)))
 
     def column_arrival(f, t):
         exists, dx, same = column_role(f)
         half = x_col.at[f, pl.ds(t * HALF, HALF), :]
         source = (dx == 0) & same
         return exists & jnp.logical_not(source), remote(
-            half, half, col_send.at[f, t, 0], col_recv.at[f, t], place(zl=1 - zl)
+            half, half, col_send.at[t, 0], col_recv.at[f, t], place(zl=1 - zl)
         )
 
     def row_role(f, q):
@@ -206,11 +213,15 @@
             return remote(half, half, sem, row_recv.at[f, q, t], where)
 
         carrier = present & same
-        yield carrier, to(row_send.at[f, q, t, 0], place(k=1 - k))
+        yield carrier, to(row_send.at[div(f, 2), q, t, 0], place(k=1 - k))
         if t == 0:
-            yield carrier & (dy != 3), to(row_send.at[f, q, t, 1], place(y=rem(y + 1, 4)))
+            direct = f < 2
+            yield carrier & ((dy == 0) | (dy == 2) | ((dy == 1) & jnp.logical_not(direct))), to(
+                row_send.at[div(f, 2), q, t, 1], place(y=rem(y + 1, 4))
+            )
+            yield carrier & (dy == 0) & direct, to(row_send.at[div(f, 2), q, t, 2], place(y=rem(y + 2, 4)))
         else:
-            yield carrier & (dy != 1), to(row_send.at[f, q, t, 1], place(y=rem(y + 3, 4)))
+            yield carrier & (dy != 1), to(row_send.at[div(f, 2), q, t, 1], place(y=rem(y + 3, 4)))
 
     def far_copies(f, q, t):
         half = x_row.at[f, q, pl.ds(t * HALF, HALF), :]
@@ -224,7 +235,7 @@
         half = x_row.at[f, q, pl.ds(t * HALF, HALF), :]
         source = (plane == zh) & (dy == 0) & same
         return present & jnp.logical_not(source), remote(
-            half, half, row_send.at[f, q, t, 0], row_recv.at[f, q, t], place(k=1 - k)
+            half, half, row_send.at[div(f, 2), q, t, 0], row_recv.at[f, q, t], place(k=1 - k)
         )
 
     def start(condition, copy):
@@ -251,41 +262,40 @@
         put_work(q, block_of(work, q) - matmul(solved, block_of(b_all, f, q)))
 
     def update(f, q):
-        early = (f == 0) | (f == 3)
 
         @pl.when(c - f + 1 < N_COL)
         def _():
-            subtract_upper(f, q, early, x_col[f])
+            subtract_upper(f, q, (f == 0) | (f == 3), x_col[f])
 
         @pl.when(8 * q + r + f - 1 >= 0)
         def _():
-            subtract_lower(f, q, early, x_row[f, q])
-
-    def bulk(f):
-        def one(q, carry):
-            done_before = owner & (q == own_slot)
-
-            @pl.when((c - 8 * q - r >= f) & jnp.logical_not(done_before))
-            def _():
-                update(f, q)
-
-            return carry
-
-        lax.fori_loop(0, N_SLOT, one, 0)
-
-    def chain_copies(distances):
-        i0 = 8 * own_slot + r
-        for by in distances:
-            later = own_front + by < FRONTS
-            f = jnp.minimum(own_front, 2)
-            yield later & (c + by < N_COL), remote(
-                x_row.at[own_front, slot], chain_row.at[f], chain_send.at[0, by - 1], chain_recv.at[0, f],
-                at_column(jnp.minimum(c + by, N_COL - 1)),
-            )
-            yield later & (i0 - by >= 0), remote(
-                x_col.at[own_front], chain_col.at[f], chain_send.at[1, by - 1], chain_recv.at[1, f],
-                at_row(rem(r + 8 - by, 8)),
-            )
+            subtract_lower(f, q, f != 1, x_row[f, q])
+
+    def bulk(f, q):
+        done_before = owner & (q == own_slot)
+
+        @pl.when((c - 8 * q - r >= f) & jnp.logical_not(done_before))
+        def _():
+            update(f, q)
+
+    def result(q):
+        return pltpu.make_async_copy(work.at[q], out_hbm.at[q], out_sem.at[q])
+
+    def chain_copies(f, row, column):
+        wanted = owner & (own_front < FRONTS - 1)
+        yield wanted & (c + 1 < N_COL), remote(
+            row, chain_row.at[f], chain_send.at[0, f], chain_recv.at[0, f], at_column(jnp.minimum(c + 1, N_COL - 1))
+        )
+        yield wanted & (8 * own_slot + r > 0), remote(
+            column, chain_col.at[f], chain_send.at[1, f], chain_recv.at[1, f], at_row(rem(r + 7, 8))
+        )
+
+    def relayed(f):
+        return chain_copies(f, chain_row.at[f], chain_col.at[f])
+
+    def own_copies():
+        f = jnp.minimum(own_front, FRONTS - 2)
+        return chain_copies(f, x_row.at[f, slot], x_col.at[f])
 
     def send_shifts(wanted):
         def one(step, carry):
@@ -296,40 +306,78 @@
 
         lax.fori_loop(0, N_SLOT, one, 0)
 
-    deferred = owner & (own_front < 2)
-    send_shifts(True)
+    mine = rem(k + r + 1, 2)
+
+    def receive_row(f, q, t, wanted):
+        arriving, arrival = row_arrival(f, q, t)
+
+        @pl.when(arriving & wanted)
+        def _():
+            with jax.named_scope(f"row#t={t}"):
+                arrival.wait_recv()
+            for condition, copy in row_copies(f, q, t):
+                start(condition, copy)
+
+    deferred = owner & (own_front < FRONTS - 1)
+    last_deferred = deferred & (own_front < 2) & (rem(own_front + r, 2) == 1)
+    beside_first = (distance == 6) & (rem(r, 2) == 0)
+    nearest = jnp.clip(zh - div(r + 7, 8) + 1, 0, N_SLOT - 1)
+    even_row = rem(r, 2) == 0
+    after_arrival = (distance == 1) | (distance == 2) | ((distance == 0) & even_row)
+    after_ring = (distance == 3) | ((distance == 4) & jnp.logical_not(even_row))
+    send_shifts(0)
+
+    @pl.when(jnp.logical_not(after_ring | (after_arrival & owner)))
+    def _():
+        send_shifts(4)
+
+    @pl.when(beside_first)
+    def _():
+        for t in (0, 1):
+            receive_row(0, nearest, t, True)
 
     @pl.when(jnp.logical_not(deferred))
     def _():
-        send_shifts(False)
+        send_shifts(1)
 
     @pl.when(owner)
     def _():
-        def earlier(f, carry):
-            @pl.when((f < own_front) & (c - f + 1 < N_COL))
+        row_first = ((k == 1) | (rem(r, 4) == 3)) & (rem(c, 8) != 0)
+
+        def earlier(step, carry):
+            f = div(step, 2)
+            take_row = (rem(step, 2) == 0) == row_first
+
+            @pl.when((f < own_front) & jnp.logical_not(take_row) & (c - f + 1 < N_COL))
             def _():
                 with jax.named_scope("chain_col"):
                     land(True, remote(chain_col.at[f], chain_col.at[f], chain_send.at[1, 0], chain_recv.at[1, f], place(k=1 - k)))
+                start(*list(relayed(f))[1])
                 with jax.named_scope("chain_upper"):
                     subtract_upper(f, slot, f != 1, chain_col[f])
 
-            @pl.when((f < own_front) & (8 * slot + r + f - 1 >= 0))
+            @pl.when((f < own_front) & take_row & (8 * slot + r + f - 1 >= 0))
             def _():
                 with jax.named_scope("chain_row"):
                     land(True, remote(chain_row.at[f], chain_row.at[f], chain_send.at[0, 0], chain_recv.at[0, f], place(k=1 - k)))
+                start(*list(relayed(f))[0])
                 with jax.named_scope("chain_lower"):
                     subtract_lower(f, slot, f != 1, chain_row[f])
 
+            @pl.when(after_arrival & (step == 0))
+            def _():
+                send_shifts(4)
+
             return carry
 
-        lax.fori_loop(0, FRONTS - 1, earlier, 0)
+        lax.fori_loop(0, 2 * (FRONTS - 1), earlier, 0)
         with jax.named_scope("solve"):
             rotated = matmul(matmul(ia[...], block_of(work, slot)), vb[...])
             solved = matmul(matmul(va[...], rotated / denominator[...]), ib[...])
             x_col[own_front] = solved
             x_row[own_front, slot] = solved
             put_work(slot, solved)
-        for condition, copy in chain_copies((1,)):
+        for condition, copy in own_copies():
             start(condition, copy)
         for t in (0, 1):
             for condition, copy in far_copies(own_front, slot, t):
@@ -339,12 +387,14 @@
                 start(condition, copy)
             for condition, copy in row_copies(own_front, slot, t):
                 start(condition, copy)
-        for condition, copy in chain_copies((2, 3)):
-            start(condition, copy)
-
-    @pl.when(deferred)
-    def _():
-        send_shifts(False)
+
+    @pl.when(deferred & jnp.logical_not(last_deferred))
+    def _():
+        send_shifts(1)
+
+    @pl.when(owner)
+    def _():
+        send_shifts(2)
 
     def receive_column(f):
         for t in (0, 1):
@@ -357,76 +407,81 @@
                 for condition, copy in column_copies(f, t):
                     start(condition, copy)
 
-    distance = rem(c - r + 32, 8)
-    relays_column = (distance >= 3) & (distance <= 5)
-
-    @pl.when(relays_column)
-    def _():
-        receive_column(jnp.clip(distance - 3, 0, FRONTS - 1))
-
-    mine = rem(k + r + 1, 2)
-
-    def receive_row(f, q, t, wanted):
-        arriving, arrival = row_arrival(f, q, t)
-
-        @pl.when(arriving & wanted)
-        def _():
-            with jax.named_scope(f"row#t={t}"):
-                arrival.wait_recv()
-            for condition, copy in row_copies(f, q, t):
-                start(condition, copy)
+    relays_column = (distance == 3) | (distance == 4)
 
     def pass_on(step, carry):
-        for arrived, forwarded, copy, arrival in passed_copies(N_SLOT - 1 - step):
-            land(arrived, arrival)
-            start(forwarded, copy)
+        arrived, forwarded, copy, arrival = passed_copy(N_SLOT - 1 - step)
+        land(arrived, arrival)
+        start(forwarded, copy)
         return carry
 
-    def ring(n, carry):
+    def ring(f):
         def one(step, carry):
-            f = mine + 2 * div(step, N_SLOT)
+            n = div(step, N_SLOT)
             q = N_SLOT - 1 - rem(step, N_SLOT)
             _, _, dy, _ = row_role(f, q)
             receive_row(f, q, 0, dy == n)
             receive_row(f, q, 1, rem(4 - dy, 4) == n)
             return carry
 
-        lax.fori_loop(0, 2 * N_SLOT, one, 0)
-
-        @pl.when(n == 1)
-        def _():
-            with jax.named_scope("pass"):
-                lax.fori_loop(0, N_SLOT, pass_on, 0)
-
+        lax.fori_loop(0, 4 * N_SLOT, one, 0)
+
+    late = (distance == 1) | (distance == 2)
+    ring(jnp.where(late, mine + 2, mine))
+
+    @pl.when(after_ring)
+    def _():
+        send_shifts(4)
+
+    @pl.when(last_deferred)
+    def _():
+        send_shifts(1)
+
+    @pl.when(jnp.logical_not(owner))
+    def _():
+        send_shifts(2)
+
+    send_shifts(3)
+
+    @pl.when(relays_column)
+    def _():
+        receive_column(distance - 3)
+
+    ring(jnp.where(late, mine, mine + 2))
+    with jax.named_scope("pass"):
+        lax.fori_loop(0, N_SLOT, pass_on, 0)
+
+    def front(f, carry):
+        opening = f == 0
+
+        @pl.when(jnp.logical_not(relays_column & (f == distance - 3)))
+        def _():
+            receive_column(f)
+
+        def one(step, carry):
+            q = N_SLOT - 1 - step
+            leaf = (rem(f, 2) != mine) & jnp.logical_not(beside_first & opening & (q == nearest))
+            for t in (0, 1):
+                receive_row(f, q, t, leaf)
+            with jax.named_scope("bulk"):
+                bulk(f, q)
+
+            @pl.when(f == FRONTS - 1)
+            def _():
+                result(q).start()
+
+            return carry
+
+        lax.fori_loop(0, N_SLOT, one, 0)
         return carry
 
-    lax.fori_loop(0, 4, ring, 0)
-
-    def front(f, carry):
-        @pl.when(jnp.logical_not(relays_column & (f == distance - 3)))
-        def _():
-            receive_column(f)
-
-        def one(q, carry):
-            for t in (0, 1):
-                receive_row(f, q, t, rem(f, 2) != mine)
-            return carry
-
-        lax.fori_loop(0, N_SLOT, one, 0)
-        with jax.named_scope("bulk"):
-            bulk(f)
-        return carry
-
     lax.fori_loop(0, FRONTS, front, 0)
-
-    result = pltpu.make_async_copy(work, out_hbm, out_sem)
-    result.start()
 
     def finish(q, carry):
         for _, condition, copy in shift_copies(q):
             drain(condition, copy)
-        for _, forwarded, copy, _ in passed_copies(q):
-            drain(forwarded, copy)
+        _, forwarded, copy, _ = passed_copy(q)
+        drain(forwarded, copy)
         return carry
 
     with jax.named_scope("finish"):
@@ -450,13 +505,22 @@
 
     @pl.when(owner)
     def _():
-        for condition, copy in chain_copies((1, 2, 3)):
+        for condition, copy in own_copies():
             drain(condition, copy)
+
+        def finish_chain(f, carry):
+            beside, above = relayed(f)
+            drain((f < own_front) & (8 * slot + r + f - 1 >= 0) & beside[0], beside[1])
+            drain((f < own_front) & (c - f + 1 < N_COL) & above[0], above[1])
+            return carry
+
+        lax.fori_loop(0, FRONTS - 1, finish_chain, 0)
         for t in (0, 1):
             for condition, copy in far_copies(own_front, slot, t):
                 drain(condition, copy)
 
-    result.wait()
+    for q in range(N_SLOT):
+        result(q).wait()
 
 
 def body(
@@ -484,15 +548,15 @@
             dma((4, N_SLOT)),
             dma((4, N_SLOT)),
             dma((4, N_SLOT)),
-            dma((FRONTS, N_SLOT, 2, 2)),
+            dma((FRONTS // 2, N_SLOT, 2, 3)),
             dma((2, 3)),
             dma((FRONTS, N_SLOT, 2)),
-            dma((FRONTS, 2, 7)),
+            dma((2, 7)),
             dma((FRONTS, 2)),
             dma((2, 3)),
             dma((2, 3)),
             dma((7,)),
-            dma,
+            dma((N_SLOT,)),
         ],
         compiler_params=pltpu.CompilerParams(
             collective_id=0, has_side_effects=True, vmem_limit_bytes=60 * 1024 * 1024

time: 115 us -> 99.5 us (0.87)
  the two profiles are of different devices: /device:TPU:229 before, /device:TPU:223 now
where the time goes in v3:
time: 99.5 us; the launch traced here: 99.3 us
  Pallas kernels  96.4 us (97%)
  local copies, waits for them, and re-layouts  2.91 us (3%)
    pallas_call x1, Pallas kernels, body(): pl.pallas_call(kernel, out_shape=jax.ShapeDtypeStruct(tall, jnp.float32),...  96.4 us
    unnamed x1, local copies, waits for them, and re-layouts  2.91 us

profile of v3, /device:TPU:223, one launch (start us, length us, event | category | flops | bytes accessed | tf_op | source)
XLA Modules:
  0.0 99.3 jit_solution(5038960819021389503)
XLA Ops:
  0.0 96.4 %shard_map.91 = f32[4,512,128]{2,1,0:T(8,128)} custom-call(f32[4,512,128]{2,1,0:T(8,128)} %bitcast.11, f32[4,512,128]{2,1,0:T(8,128)} %bitcast.12, f32[4,512,128]{2,1,0:T(8,128)} %bitcast.13, f32[4,256,256]{2,1,0:T(8,128)} %bitcast.14, f32[4,256,256]{2,1,0:T(8,128)} %bitcast.15, f32[8,128]{1,0:T(8,128)} %bitcast.18, f32[256,256]{1,0:T(8,128)} %bitcast.16, ...), custom_call_target="tpu_custom_call" | custom-call | tf_op jit(solution)/shard_map/pallas_call | solution.py:534
  96.4 2.9 %copy.12 = f32[4,1,256,1,256]{4,3,2,1,0:T(1,128)} copy(f32[4,1,256,1,256]{4,3,2,1,0:T(1,128)} %bitcast.10) | data formatting | bytes 2097152

commit v4 on v3

--- a/solution.py
+++ b/solution.py
@@ -33,9 +33,9 @@
 
 
 def kernel(
-    a_hbm, b_hbm, w_hbm, va_hbm, ia_hbm, la_ref, vb_hbm, ib_hbm, lb_ref, out_hbm,
-    a_all, b_all, work, x_col, x_row, chain_col, chain_row, va, ia, vb, ib, denominator,
-    a_send, a_recv, b_send, b_recv, row_send, row_far, row_recv, col_send, col_recv, chain_send, chain_recv, local, out_sem,
+    a_hbm, b_hbm, w_hbm, va_hbm, ia_hbm, la_ref, vb_hbm, ib_hbm, lb_ref, work,
+    a_all, b_all, x_col, x_row, chain_col, chain_row, va, ia, vb, ib, denominator,
+    a_send, a_recv, b_send, b_recv, row_send, row_far, row_recv, col_send, col_recv, chain_send, chain_recv, local,
 ):
     zl, x = lax.axis_index("zl"), lax.axis_index("x")
     zh, y, k = lax.axis_index("zh"), lax.axis_index("y"), lax.axis_index("k")
@@ -125,7 +125,7 @@
         above = 8 * q + r < c
         near = (q == near_slot) & (distance >= 1) & (distance <= 3)
         nearer = near & (distance == 1)
-        crossing = (rem(c, 8) >= 6) & (x != 1)
+        crossing = (rem(c, 8) >= 6) & (x != 1) & ((x == 0) | (zl == 1))
         first_row = jnp.where(r == 0, 1, 0)
         second_row = jnp.where(r <= 1, 1, 0)
         left = at_column(jnp.maximum(c - 1, 0))
@@ -157,7 +157,7 @@
         wanted = above & (c + 2 < N_COL) & (k == 0)
         yield 1, wanted & jnp.logical_not(crossing), a_copy(3, farther)
         yield 2, wanted & crossing, a_copy(3, farther)
-        yield 3, above & (8 * q + r >= 2), b_copy(3, q - second_row, highest)
+        yield 3, above & (x >= 2), b_copy(3, q - second_row, highest)
 
     def passed_copy(q):
         fresh = jnp.logical_not(owner & (own_front == 3) & (q == own_slot))
@@ -165,6 +165,16 @@
         return here & fresh, here & (k == 0), remote(
             a_all.at[2, q], a_all.at[3, q], a_send.at[1, q], a_recv.at[3, q], place(k=1 - k)
         ), remote(a_all.at[2, q], a_all.at[2, q], a_send.at[2, q], a_recv.at[2, q], place(k=1 - k))
+
+    hands_on = (x == 0) | (x == 3)
+
+    def handed_copy(q):
+        fresh = jnp.logical_not(owner & (own_front == 3) & (q == own_slot))
+        here = hands_on & (8 * q + r + 1 < c)
+        down_slot = jnp.maximum(q - jnp.where(r == 0, 1, 0), 0)
+        return here & fresh, here & (8 * q + r > 0), remote(
+            b_all.at[2, q], b_all.at[3, down_slot], b_send.at[1, q], b_recv.at[3, down_slot], at_row(rem(r + 7, 8))
+        ), remote(b_all.at[2, q], b_all.at[2, q], b_send.at[2, q], b_recv.at[2, q], place(k=1 - k))
 
     def column_role(f):
         i0 = c - f + 1
@@ -182,12 +192,11 @@
             return remote(half, half, col_send.at[t, n], col_recv.at[f, t], where)
 
         source = exists & (dx == 0) & same
-        twin = exists & (dx == 0) & jnp.logical_not(same) & (f < 2)
         yield source, to(3, place(zl=1 - zl))
         for by in (3, 1, 2):
-            yield source | twin, to(by - 1, place(x=rem(x + by, 4)))
+            yield source, to(by - 1, place(x=rem(x + by, 4)))
         for by in (3, 1, 2):
-            yield source & (f >= 2), to(3 + by, place(zl=1 - zl, x=rem(x + by, 4)))
+            yield source, to(3 + by, place(zl=1 - zl, x=rem(x + by, 4)))
 
     def column_arrival(f, t):
         exists, dx, same = column_role(f)
@@ -253,33 +262,54 @@
         def _():
             copy.wait_recv()
 
-    def subtract_upper(f, q, arrived, solved):
-        land(arrived, remote(a_all.at[f, q], a_all.at[f, q], a_send.at[f, q], a_recv.at[f, q], place(k=1 - k)))
+    def land_a(f, q, wanted):
+        land(wanted, remote(a_all.at[f, q], a_all.at[f, q], a_send.at[f, q], a_recv.at[f, q], place(k=1 - k)))
+
+    def land_b(f, q, wanted):
+        land(wanted, remote(b_all.at[f, q], b_all.at[f, q], b_send.at[f, q], b_recv.at[f, q], place(k=1 - k)))
+
+    def subtract_upper(f, q, solved):
         put_work(q, block_of(work, q) - matmul(block_of(a_all, f, q), solved))
 
-    def subtract_lower(f, q, arrived, solved):
-        land(arrived, remote(b_all.at[f, q], b_all.at[f, q], b_send.at[f, q], b_recv.at[f, q], place(k=1 - k)))
+    def subtract_lower(f, q, solved):
         put_work(q, block_of(work, q) - matmul(solved, block_of(b_all, f, q)))
 
     def update(f, q):
-
-        @pl.when(c - f + 1 < N_COL)
+        ahead = c - 8 * q - r
+        open_block = jnp.logical_not(owner & (q == own_slot))
+        upper = c - f + 1 < N_COL
+        lower = 8 * q + r + f - 1 >= 0
+        both = open_block & (ahead >= f + 1) & upper & lower
+        for g, pending in ((f, open_block & (ahead >= f)), (f + 1, open_block & (ahead >= f + 1))):
+            land_a(g, q, pending & (c - g + 1 < N_COL) & ((g == 0) | (g == 3)))
+            land_b(
+                g, q, pending & (8 * q + r + g - 1 >= 0) & ((g == 0) | (g == 3) | ((g == 2) & jnp.logical_not(hands_on)))
+            )
+
+        @pl.when(both)
         def _():
-            subtract_upper(f, q, (f == 0) | (f == 3), x_col[f])
-
-        @pl.when(8 * q + r + f - 1 >= 0)
-        def _():
-            subtract_lower(f, q, f != 1, x_row[f, q])
-
-    def bulk(f, q):
-        done_before = owner & (q == own_slot)
-
-        @pl.when((c - 8 * q - r >= f) & jnp.logical_not(done_before))
-        def _():
-            update(f, q)
-
-    def result(q):
-        return pltpu.make_async_copy(work.at[q], out_hbm.at[q], out_sem.at[q])
+            left = jnp.concatenate(
+                [block_of(a_all, f, q), block_of(a_all, f + 1, q), x_row[f, q], x_row[f + 1, q]], axis=1
+            )
+            right = jnp.concatenate(
+                [x_col[f], x_col[f + 1], block_of(b_all, f, q), block_of(b_all, f + 1, q)], axis=0
+            )
+            put_work(q, block_of(work, q) - matmul(left, right))
+
+        def one(g, carry):
+            pending = open_block & jnp.logical_not(both) & (ahead >= g)
+
+            @pl.when(pending & (c - g + 1 < N_COL))
+            def _():
+                subtract_upper(g, q, x_col[g])
+
+            @pl.when(pending & (8 * q + r + g - 1 >= 0))
+            def _():
+                subtract_lower(g, q, x_row[g, q])
+
+            return carry
+
+        lax.fori_loop(f, f + 2, one, 0)
 
     def chain_copies(f, row, column):
         wanted = owner & (own_front < FRONTS - 1)
@@ -319,26 +349,43 @@
                 start(condition, copy)
 
     deferred = owner & (own_front < FRONTS - 1)
-    last_deferred = deferred & (own_front < 2) & (rem(own_front + r, 2) == 1)
-    beside_first = (distance == 6) & (rem(r, 2) == 0)
-    nearest = jnp.clip(zh - div(r + 7, 8) + 1, 0, N_SLOT - 1)
     even_row = rem(r, 2) == 0
-    after_arrival = (distance == 1) | (distance == 2) | ((distance == 0) & even_row)
-    after_ring = (distance == 3) | ((distance == 4) & jnp.logical_not(even_row))
+    after_arrival = owner & ((distance == 1) | (distance == 2) | ((distance == 0) & even_row))
+    fourth = (distance == 4) & (k == 1)
+    beside = ((k == 0) & ((distance == 6) | (distance == 7) | (distance == 0))) | fourth
+    beside_front = jnp.where(beside & jnp.logical_not(fourth), rem(distance + 2, 8), 0)
+    nearest = zh - div(r + beside_front + 7, 8) + 1
+    watches = beside & (nearest >= 0) & (nearest < N_SLOT)
+    watched = jnp.clip(nearest, 0, N_SLOT - 1)
+
+    def watch():
+        for t in (0, 1):
+            receive_row(beside_front, watched, t, True)
+
+    solves_later = (distance == 7) | (distance == 0)
     send_shifts(0)
 
-    @pl.when(jnp.logical_not(after_ring | (after_arrival & owner)))
+    @pl.when(jnp.logical_not(after_arrival | fourth))
     def _():
         send_shifts(4)
 
-    @pl.when(beside_first)
-    def _():
-        for t in (0, 1):
-            receive_row(0, nearest, t, True)
+    @pl.when(watches & jnp.logical_not(solves_later))
+    def _():
+        watch()
+
+    @pl.when(fourth)
+    def _():
+        send_shifts(4)
+
+    middle = (distance >= 3) & (distance <= 5)
 
     @pl.when(jnp.logical_not(deferred))
     def _():
         send_shifts(1)
+
+    @pl.when(middle)
+    def _():
+        send_shifts(3)
 
     @pl.when(owner)
     def _():
@@ -354,7 +401,8 @@
                     land(True, remote(chain_col.at[f], chain_col.at[f], chain_send.at[1, 0], chain_recv.at[1, f], place(k=1 - k)))
                 start(*list(relayed(f))[1])
                 with jax.named_scope("chain_upper"):
-                    subtract_upper(f, slot, f != 1, chain_col[f])
+                    land_a(f, slot, f != 1)
+                    subtract_upper(f, slot, chain_col[f])
 
             @pl.when((f < own_front) & take_row & (8 * slot + r + f - 1 >= 0))
             def _():
@@ -362,7 +410,8 @@
                     land(True, remote(chain_row.at[f], chain_row.at[f], chain_send.at[0, 0], chain_recv.at[0, f], place(k=1 - k)))
                 start(*list(relayed(f))[0])
                 with jax.named_scope("chain_lower"):
-                    subtract_lower(f, slot, f != 1, chain_row[f])
+                    land_b(f, slot, f != 1)
+                    subtract_lower(f, slot, chain_row[f])
 
             @pl.when(after_arrival & (step == 0))
             def _():
@@ -388,32 +437,36 @@
             for condition, copy in row_copies(own_front, slot, t):
                 start(condition, copy)
 
-    @pl.when(deferred & jnp.logical_not(last_deferred))
+    @pl.when(watches & solves_later)
+    def _():
+        watch()
+
+    @pl.when(deferred)
     def _():
         send_shifts(1)
 
     @pl.when(owner)
     def _():
         send_shifts(2)
+
+    @pl.when(jnp.logical_not(middle))
+    def _():
+        send_shifts(3)
 
     def receive_column(f):
         for t in (0, 1):
-            arriving, arrival = column_arrival(f, t)
-
-            @pl.when(arriving)
-            def _():
-                with jax.named_scope(f"col#t={t}"):
-                    arrival.wait_recv()
-                for condition, copy in column_copies(f, t):
-                    start(condition, copy)
-
-    relays_column = (distance == 3) | (distance == 4)
-
-    def pass_on(step, carry):
-        arrived, forwarded, copy, arrival = passed_copy(N_SLOT - 1 - step)
-        land(arrived, arrival)
-        start(forwarded, copy)
-        return carry
+            with jax.named_scope(f"col#t={t}"):
+                land(*column_arrival(f, t))
+
+    def pass_on(which):
+        def one(step, carry):
+            arrived, forwarded, copy, arrival = which(N_SLOT - 1 - step)
+            land(arrived, arrival)
+            start(forwarded, copy)
+            return carry
+
+        with jax.named_scope("pass"):
+            lax.fori_loop(0, N_SLOT, one, 0)
 
     def ring(f):
         def one(step, carry):
@@ -429,59 +482,49 @@
     late = (distance == 1) | (distance == 2)
     ring(jnp.where(late, mine + 2, mine))
 
-    @pl.when(after_ring)
-    def _():
-        send_shifts(4)
-
-    @pl.when(last_deferred)
-    def _():
-        send_shifts(1)
-
     @pl.when(jnp.logical_not(owner))
     def _():
         send_shifts(2)
 
-    send_shifts(3)
-
-    @pl.when(relays_column)
-    def _():
-        receive_column(distance - 3)
-
-    ring(jnp.where(late, mine, mine + 2))
-    with jax.named_scope("pass"):
-        lax.fori_loop(0, N_SLOT, pass_on, 0)
-
-    def front(f, carry):
-        opening = f == 0
-
-        @pl.when(jnp.logical_not(relays_column & (f == distance - 3)))
-        def _():
-            receive_column(f)
+    pass_on(handed_copy)
+
+    def pair(f):
+        for g in (f, f + 1):
+            receive_column(g)
 
         def one(step, carry):
             q = N_SLOT - 1 - step
-            leaf = (rem(f, 2) != mine) & jnp.logical_not(beside_first & opening & (q == nearest))
-            for t in (0, 1):
-                receive_row(f, q, t, leaf)
+            for g in (f, f + 1):
+                leaf = (rem(g, 2) != mine) & jnp.logical_not(watches & (g == beside_front) & (q == nearest))
+                for t in (0, 1):
+                    receive_row(g, q, t, leaf)
             with jax.named_scope("bulk"):
-                bulk(f, q)
-
-            @pl.when(f == FRONTS - 1)
-            def _():
-                result(q).start()
-
+                update(f, q)
             return carry
 
         lax.fori_loop(0, N_SLOT, one, 0)
+
+    early = (mine == 1) & ((distance == 0) | (distance >= 4)) & (x != 0) & (rem(c, 8) != 7)
+
+    def stage(j, carry):
+        @pl.when(j == 1)
+        def _():
+            ring(jnp.where(late, mine, mine + 2))
+            pass_on(passed_copy)
+
+        @pl.when((j == 3) | ((j == 0) & early) | ((j == 2) & jnp.logical_not(early)))
+        def _():
+            pair(jnp.where(j == 3, 2, 0))
+
         return carry
 
-    lax.fori_loop(0, FRONTS, front, 0)
+    lax.fori_loop(0, 4, stage, 0)
 
     def finish(q, carry):
         for _, condition, copy in shift_copies(q):
             drain(condition, copy)
-        _, forwarded, copy, _ = passed_copy(q)
-        drain(forwarded, copy)
+        for _, forwarded, copy, _ in (passed_copy(q), handed_copy(q)):
+            drain(forwarded, copy)
         return carry
 
     with jax.named_scope("finish"):
@@ -518,9 +561,6 @@
         for t in (0, 1):
             for condition, copy in far_copies(own_front, slot, t):
                 drain(condition, copy)
-
-    for q in range(N_SLOT):
-        result(q).wait()
 
 
 def body(
@@ -533,13 +573,12 @@
     dma = pltpu.SemaphoreType.DMA
     solved = pl.pallas_call(
         kernel,
-        out_shape=jax.ShapeDtypeStruct(tall, jnp.float32),
+        out_shape=pltpu.VMEM(tall, jnp.float32),
         in_specs=[anywhere] * 5 + [inside] + [anywhere] * 2 + [inside],
-        out_specs=anywhere,
+        out_specs=inside,
         scratch_shapes=[
             pltpu.VMEM((FRONTS, *tall), jnp.float32),
             pltpu.VMEM((FRONTS, *tall), jnp.float32),
-            pltpu.VMEM(tall, jnp.float32),
             pltpu.VMEM(square, jnp.float32),
             pltpu.VMEM((FRONTS, *square), jnp.float32),
             *[pltpu.VMEM((FRONTS - 1, BLOCK, BLOCK), jnp.float32)] * 2,
@@ -556,7 +595,6 @@
             dma((2, 3)),
             dma((2, 3)),
             dma((7,)),
-            dma((N_SLOT,)),
         ],
         compiler_params=pltpu.CompilerParams(
             collective_id=0, has_side_effects=True, vmem_limit_bytes=60 * 1024 * 1024

time: 99.5 us -> 94.4 us (0.949)
  the two profiles are of different devices: /device:TPU:223 before, /device:TPU:165 now
where the time goes in v4:
time: 94.4 us; the launch traced here: 94.3 us
  Pallas kernels  93.3 us (99%)
  local copies, waits for them, and re-layouts  0.97 us (1%)
    pallas_call x1, Pallas kernels, body(): pl.pallas_call(kernel, out_shape=pltpu.VMEM(tall, jnp.float32), in_specs=...  93.3 us

profile of v4, /device:TPU:165, one launch (start us, length us, event | category | flops | bytes accessed | tf_op | source)
XLA Modules:
  0.0 94.3 jit_solution(12921593270382298957)
XLA Ops:
  0.0 93.3 %shard_map.91 = f32[4,512,128]{2,1,0:T(8,128)S(1)} custom-call(f32[4,512,128]{2,1,0:T(8,128)} %bitcast.11, f32[4,512,128]{2,1,0:T(8,128)} %bitcast.12, f32[4,512,128]{2,1,0:T(8,128)} %bitcast.13, f32[4,256,256]{2,1,0:T(8,128)} %bitcast.14, f32[4,256,256]{2,1,0:T(8,128)} %bitcast.15, f32[8,128]{1,0:T(8,128)} %bitcast.18, f32[256,256]{1,0:T(8,128)} %bitcast.16, ...), custom_call_target="tpu_custom_call" | custom-call | tf_op jit(solution)/shard_map/pallas_call | solution.py:574
  93.3 1.0 %copy.12 = f32[4,1,256,1,256]{4,3,2,1,0:T(1,128)} copy(f32[4,1,256,1,256]{4,3,2,1,0:T(1,128)S(1)} %bitcast.10) | data formatting | bytes 2097152

commit v5 on v4

--- a/solution.py
+++ b/solution.py
@@ -34,7 +34,7 @@
 
 def kernel(
     a_hbm, b_hbm, w_hbm, va_hbm, ia_hbm, la_ref, vb_hbm, ib_hbm, lb_ref, work,
-    a_all, b_all, x_col, x_row, chain_col, chain_row, va, ia, vb, ib, denominator,
+    a_all, b_all, x_col, x_row, chain_row, va, ia, vb, ib, denominator,
     a_send, a_recv, b_send, b_recv, row_send, row_far, row_recv, col_send, col_recv, chain_send, chain_recv, local,
 ):
     zl, x = lax.axis_index("zl"), lax.axis_index("x")
@@ -192,17 +192,18 @@
             return remote(half, half, col_send.at[t, n], col_recv.at[f, t], where)
 
         source = exists & (dx == 0) & same
-        yield source, to(3, place(zl=1 - zl))
-        for by in (3, 1, 2):
-            yield source, to(by - 1, place(x=rem(x + by, 4)))
-        for by in (3, 1, 2):
-            yield source, to(3 + by, place(zl=1 - zl, x=rem(x + by, 4)))
+        for n in range(7):
+            there_zl = zl if n < 3 else 1 - zl
+            there_x = rem(x + (3, 1, 2, 0, 3, 1, 2)[n], 4)
+            apart = rem(r - there_zl * 4 - there_x + 8, 8)
+            chained = (apart <= FRONTS - 1 - f) & (c - f + 1 - apart >= 0)
+            yield source & jnp.logical_not(chained), to(n, place(zl=there_zl, x=there_x))
 
     def column_arrival(f, t):
         exists, dx, same = column_role(f)
         half = x_col.at[f, pl.ds(t * HALF, HALF), :]
         source = (dx == 0) & same
-        return exists & jnp.logical_not(source), remote(
+        return exists & jnp.logical_not(source | (owner & (own_front > f))), remote(
             half, half, col_send.at[t, 0], col_recv.at[f, t], place(zl=1 - zl)
         )
 
@@ -317,11 +318,11 @@
             row, chain_row.at[f], chain_send.at[0, f], chain_recv.at[0, f], at_column(jnp.minimum(c + 1, N_COL - 1))
         )
         yield wanted & (8 * own_slot + r > 0), remote(
-            column, chain_col.at[f], chain_send.at[1, f], chain_recv.at[1, f], at_row(rem(r + 7, 8))
+            column, x_col.at[f], chain_send.at[1, f], chain_recv.at[1, f], at_row(rem(r + 7, 8))
         )
 
     def relayed(f):
-        return chain_copies(f, chain_row.at[f], chain_col.at[f])
+        return chain_copies(f, chain_row.at[f], x_col.at[f])
 
     def own_copies():
         f = jnp.minimum(own_front, FRONTS - 2)
@@ -352,7 +353,7 @@
     even_row = rem(r, 2) == 0
     after_arrival = owner & ((distance == 1) | (distance == 2) | ((distance == 0) & even_row))
     fourth = (distance == 4) & (k == 1)
-    beside = ((k == 0) & ((distance == 6) | (distance == 7) | (distance == 0))) | fourth
+    beside = ((k == 0) & ((distance == 6) | (distance == 7) | ((distance == 0) & (x != 0)))) | fourth
     beside_front = jnp.where(beside & jnp.logical_not(fourth), rem(distance + 2, 8), 0)
     nearest = zh - div(r + beside_front + 7, 8) + 1
     watches = beside & (nearest >= 0) & (nearest < N_SLOT)
@@ -398,11 +399,11 @@
             @pl.when((f < own_front) & jnp.logical_not(take_row) & (c - f + 1 < N_COL))
             def _():
                 with jax.named_scope("chain_col"):
-                    land(True, remote(chain_col.at[f], chain_col.at[f], chain_send.at[1, 0], chain_recv.at[1, f], place(k=1 - k)))
+                    land(True, remote(x_col.at[f], x_col.at[f], chain_send.at[1, 0], chain_recv.at[1, f], place(k=1 - k)))
                 start(*list(relayed(f))[1])
                 with jax.named_scope("chain_upper"):
                     land_a(f, slot, f != 1)
-                    subtract_upper(f, slot, chain_col[f])
+                    subtract_upper(f, slot, x_col[f])
 
             @pl.when((f < own_front) & take_row & (8 * slot + r + f - 1 >= 0))
             def _():
@@ -581,7 +582,7 @@
             pltpu.VMEM((FRONTS, *tall), jnp.float32),
             pltpu.VMEM(square, jnp.float32),
             pltpu.VMEM((FRONTS, *square), jnp.float32),
-            *[pltpu.VMEM((FRONTS - 1, BLOCK, BLOCK), jnp.float32)] * 2,
+            pltpu.VMEM((FRONTS - 1, BLOCK, BLOCK), jnp.float32),
             *[pltpu.VMEM((BLOCK, BLOCK), jnp.float32)] * 5,
             dma((4, N_SLOT)),
             dma((4, N_SLOT)),

time: 94.4 us -> 92 us (0.975)
  the two profiles are of different devices: /device:TPU:165 before, /device:TPU:192 now
where the time goes in v5:
time: 92 us; the launch traced here: 90.4 us
  Pallas kernels  89.4 us (97%)
  local copies, waits for them, and re-layouts  0.97 us (1%)
    pallas_call x1, Pallas kernels, body(): pl.pallas_call(kernel, out_shape=pltpu.VMEM(tall, jnp.float32), in_specs=...  89.4 us

profile of v5, /device:TPU:192, one launch (start us, length us, event | category | flops | bytes accessed | tf_op | source)
XLA Modules:
  0.0 90.4 jit_solution(3652099906079455973)
XLA Ops:
  0.0 89.4 %shard_map.91 = f32[4,512,128]{2,1,0:T(8,128)S(1)} custom-call(f32[4,512,128]{2,1,0:T(8,128)} %bitcast.11, f32[4,512,128]{2,1,0:T(8,128)} %bitcast.12, f32[4,512,128]{2,1,0:T(8,128)} %bitcast.13, f32[4,256,256]{2,1,0:T(8,128)} %bitcast.14, f32[4,256,256]{2,1,0:T(8,128)} %bitcast.15, f32[8,128]{1,0:T(8,128)} %bitcast.18, f32[256,256]{1,0:T(8,128)} %bitcast.16, ...), custom_call_target="tpu_custom_call" | custom-call | tf_op jit(solution)/shard_map/pallas_call | solution.py:575
  89.4 1.0 %copy.12 = f32[4,1,256,1,256]{4,3,2,1,0:T(1,128)} copy(f32[4,1,256,1,256]{4,3,2,1,0:T(1,128)S(1)} %bitcast.10) | data formatting | bytes 2097152

commit v6 on v5

--- a/solution.py
+++ b/solution.py
@@ -157,7 +157,7 @@
         wanted = above & (c + 2 < N_COL) & (k == 0)
         yield 1, wanted & jnp.logical_not(crossing), a_copy(3, farther)
         yield 2, wanted & crossing, a_copy(3, farther)
-        yield 3, above & (x >= 2), b_copy(3, q - second_row, highest)
+        yield 3, above & (x == 2), b_copy(3, q - second_row, highest)
 
     def passed_copy(q):
         fresh = jnp.logical_not(owner & (own_front == 3) & (q == own_slot))
@@ -166,7 +166,7 @@
             a_all.at[2, q], a_all.at[3, q], a_send.at[1, q], a_recv.at[3, q], place(k=1 - k)
         ), remote(a_all.at[2, q], a_all.at[2, q], a_send.at[2, q], a_recv.at[2, q], place(k=1 - k))
 
-    hands_on = (x == 0) | (x == 3)
+    hands_on = x != 1
 
     def handed_copy(q):
         fresh = jnp.logical_not(owner & (own_front == 3) & (q == own_slot))
@@ -349,7 +349,7 @@
             for condition, copy in row_copies(f, q, t):
                 start(condition, copy)
 
-    deferred = owner & (own_front < FRONTS - 1)
+    deferred = owner & (own_front < FRONTS - 2)
     even_row = rem(r, 2) == 0
     after_arrival = owner & ((distance == 1) | (distance == 2) | ((distance == 0) & even_row))
     fourth = (distance == 4) & (k == 1)
@@ -446,7 +446,9 @@
     def _():
         send_shifts(1)
 
-    @pl.when(owner)
+    crosses_soon = owner | ((r == 0) & (distance == 6))
+
+    @pl.when(crosses_soon)
     def _():
         send_shifts(2)
 
@@ -469,25 +471,34 @@
         with jax.named_scope("pass"):
             lax.fori_loop(0, N_SLOT, one, 0)
 
-    def ring(f):
+    soon = (x >= 2) & (distance >= 3) & (distance <= 6)
+
+    def ring(f, opening):
         def one(step, carry):
             n = div(step, N_SLOT)
             q = N_SLOT - 1 - rem(step, N_SLOT)
             _, _, dy, _ = row_role(f, q)
             receive_row(f, q, 0, dy == n)
             receive_row(f, q, 1, rem(4 - dy, 4) == n)
+
+            @pl.when(soon & opening & (step == 2 * N_SLOT - 1))
+            def _():
+                pass_on(handed_copy)
+
             return carry
 
         lax.fori_loop(0, 4 * N_SLOT, one, 0)
 
     late = (distance == 1) | (distance == 2)
-    ring(jnp.where(late, mine + 2, mine))
-
-    @pl.when(jnp.logical_not(owner))
+    ring(jnp.where(late, mine + 2, mine), True)
+
+    @pl.when(jnp.logical_not(crosses_soon))
     def _():
         send_shifts(2)
 
-    pass_on(handed_copy)
+    @pl.when(jnp.logical_not(soon))
+    def _():
+        pass_on(handed_copy)
 
     def pair(f):
         for g in (f, f + 1):
@@ -510,7 +521,7 @@
     def stage(j, carry):
         @pl.when(j == 1)
         def _():
-            ring(jnp.where(late, mine, mine + 2))
+            ring(jnp.where(late, mine, mine + 2), False)
             pass_on(passed_copy)
 
         @pl.when((j == 3) | ((j == 0) & early) | ((j == 2) & jnp.logical_not(early)))

time: 92 us -> 85 us (0.924); the launches traced: 90.4 us -> 84.5 us
  Pallas kernels: 89.4 us -> 83.5 us
    pallas_call x1, Pallas kernels: 89.4 us -> 83.5 us  [body(): pl.pallas_call(kernel, out_shape=pltpu.VMEM(tall, jnp.float32), in_specs=...]
where the time goes in v6:
time: 85 us; the launch traced here: 84.5 us
  Pallas kernels  83.5 us (98%)
  local copies, waits for them, and re-layouts  0.97 us (1%)
    pallas_call x1, Pallas kernels, body(): pl.pallas_call(kernel, out_shape=pltpu.VMEM(tall, jnp.float32), in_specs=...  83.5 us

profile of v6, /device:TPU:192, one launch (start us, length us, event | category | flops | bytes accessed | tf_op | source)
XLA Modules:
  0.0 84.5 jit_solution(12157638359477240991)
XLA Ops:
  0.0 83.5 %shard_map.91 = f32[4,512,128]{2,1,0:T(8,128)S(1)} custom-call(f32[4,512,128]{2,1,0:T(8,128)} %bitcast.11, f32[4,512,128]{2,1,0:T(8,128)} %bitcast.12, f32[4,512,128]{2,1,0:T(8,128)} %bitcast.13, f32[4,256,256]{2,1,0:T(8,128)} %bitcast.14, f32[4,256,256]{2,1,0:T(8,128)} %bitcast.15, f32[8,128]{1,0:T(8,128)} %bitcast.18, f32[256,256]{1,0:T(8,128)} %bitcast.16, ...), custom_call_target="tpu_custom_call" | custom-call | tf_op jit(solution)/shard_map/pallas_call | solution.py:586
  83.5 1.0 %copy.12 = f32[4,1,256,1,256]{4,3,2,1,0:T(1,128)} copy(f32[4,1,256,1,256]{4,3,2,1,0:T(1,128)S(1)} %bitcast.10) | data formatting | bytes 2097152

commit v7 on v6

--- a/solution.py
+++ b/solution.py
@@ -446,7 +446,7 @@
     def _():
         send_shifts(1)
 
-    crosses_soon = owner | ((r == 0) & (distance == 6))
+    crosses_soon = owner | ((r == 0) & (distance == 6)) | ((r == 2) | (r == 3))
 
     @pl.when(crosses_soon)
     def _():

time: 85 us -> 85 us (level)
  no operation moved by 1% of the time
where the time goes in v7:
time: 85 us; the launch traced here: 84.5 us
  Pallas kernels  83.5 us (98%)
  local copies, waits for them, and re-layouts  0.97 us (1%)
    pallas_call x1, Pallas kernels, body(): pl.pallas_call(kernel, out_shape=pltpu.VMEM(tall, jnp.float32), in_specs=...  83.5 us

profile of v7, /device:TPU:192, one launch (start us, length us, event | category | flops | bytes accessed | tf_op | source)
XLA Modules:
  0.0 84.5 jit_solution(3763124615522491502)
XLA Ops:
  0.0 83.5 %shard_map.91 = f32[4,512,128]{2,1,0:T(8,128)S(1)} custom-call(f32[4,512,128]{2,1,0:T(8,128)} %bitcast.11, f32[4,512,128]{2,1,0:T(8,128)} %bitcast.12, f32[4,512,128]{2,1,0:T(8,128)} %bitcast.13, f32[4,256,256]{2,1,0:T(8,128)} %bitcast.14, f32[4,256,256]{2,1,0:T(8,128)} %bitcast.15, f32[8,128]{1,0:T(8,128)} %bitcast.18, f32[256,256]{1,0:T(8,128)} %bitcast.16, ...), custom_call_target="tpu_custom_call" | custom-call | tf_op jit(solution)/shard_map/pallas_call | solution.py:586
  83.5 1.0 %copy.12 = f32[4,1,256,1,256]{4,3,2,1,0:T(1,128)} copy(f32[4,1,256,1,256]{4,3,2,1,0:T(1,128)S(1)} %bitcast.10) | data formatting | bytes 2097152
